TPU v7x, 256 devices: a whole 4x4x8 slice. The times are simulated.
256 devices in a mesh: grp: 16 (over x, y), dev: 16 (over z, core).
Axes of the slice: x: 4, y: 4, z: 8, core: 2. Of those that a mesh axis runs over, the one named last changes fastest.
Arguments:
- q_lat: bfloat16 [1024, 64, 576], P(('grp', 'dev')), parts along dimension 0, may hold values from -40 to 40
- latent_cache: bfloat16 [1024, 256, 576], P(('grp', 'dev')), parts along dimension 0, may hold values from -8 to 8
- lengths: int32 [1024], P('grp'), parts along dimension 0, may hold values from 32 to 256, as said below
- moves: int32 [512, 3], P('grp'), parts along dimension 0, may hold values from 0 to 63, as said below
- hidden_in: bfloat16 [1024, 3584], P(('grp', 'dev')), parts along dimension 0, may hold values from -6 to 6
- norm_gain: bfloat16 [3584], replicated, may hold values from 0.25 to 1.75
- w_up: bfloat16 [3584, 10240], P(None, 'dev'), may hold values from -0.09375 to 0.09375
- w_down: bfloat16 [10240, 3584], P('dev'), may hold values from -0.0625 to 0.0625
- queue_counts: int32 [256, 8], P(('grp', 'dev')), parts along dimension 0, may hold values from 0 to 63
- deadline: int32 [1024], P(('grp', 'dev')), parts along dimension 0, may hold values from 0 to 7
Outputs:
- attn_out: bfloat16 [1024, 64, 512], P(('grp', 'dev')), parts along dimension 0
- new_cache: bfloat16 [1024, 256, 576], P(('grp', 'dev')), parts along dimension 0
- mixed: bfloat16 [1024, 3584], P(('grp', 'dev')), parts along dimension 0
- bucket_load: float32 [128], P('grp'), parts along dimension 0
There are 16 independent parts, one for each index of `grp`. A program takes and returns all parts, laid end to end along the dimension named above; an argument that names none is the same for every part. Nothing has to cross between parts.
Inputs may be any that keep to these rules, and one draw needn't show every extreme that they name: `lengths`: every length is at least 32; some request has exactly 256. `moves`: entry j * 16 + s (j below 2) has source device s and names a request of device s (requests r lie on device r // 4); the requests listed for one device are distinct. In round j every source s sends to (s + k_j) mod 16, with k_j between 1 and 15 the same for all sources of the round and different between rounds; one of the rounds has k_j = 8.
All inputs are finite; a program needn't handle non-finite values.
Results may differ from a plain program's by a relative error of at most 0.002.
The roundings to bfloat16 on the way count: a program that leaves them out, or rounds other values in their place, can miss the bound.
Values may be sent and summed in bfloat16 or wider, within the bound.
No kernel may reach another device: no remote copies, remote signals or barrier semaphores. Data moves between devices by JAX's collectives and lax.ppermute only.
A program may use at most 128 MiB of HBM per device.

v0:
```python
from functools import partial

import jax
import jax.numpy as jnp
from jax import lax
from jax.sharding import PartitionSpec as P

VL = 512
MOVE_DEV = 2
BUCKETS = 8


softmax_scale = 192.0 ** (-0.5)


def for_sending(x):

    def short(part):
        return part.astype(jnp.bfloat16) if part.dtype == jnp.float32 else part

    return jax.tree.map(short, x)


def shifted(value, axis, steps):
    count = lax.axis_size(axis)
    pairs = [(source, (source + steps) % count) for source in range(count)]
    return lax.ppermute(value, axis, pairs)


def in_order(tiles, dim):
    tiles = jnp.moveaxis(tiles, 0, dim)
    dims = tiles.shape
    return tiles.reshape(*dims[:dim], dims[dim] * dims[dim + 1], *dims[dim + 2 :])


def sent_to_all(x, axis):
    peers = lax.axis_size(axis)
    return lax.all_to_all(jnp.broadcast_to(x[None], (peers, *x.shape)), axis, 0, 0, tiled=True)


def collect(x, axis, dim):
    return in_order(sent_to_all(x, axis), dim)


def taken_together(x, axis):
    return sent_to_all(x, axis).sum(axis=0)


def split_up(x, dim, peers):
    dims = x.shape
    tiles = x.reshape(*dims[:dim], peers, dims[dim] // peers, *dims[dim + 1 :])
    return jnp.moveaxis(tiles, dim, 0)


def sum_at_owner(x, axis, dim):
    tiles = split_up(x, dim, lax.axis_size(axis))
    arrived = lax.all_to_all(tiles, axis, split_axis=0, concat_axis=0, tiled=True)
    return arrived.sum(axis=0)


def attend(queries, latent, context_lengths):
    row_count = queries.shape[0]
    head_count = queries.shape[1]
    block_size = min(128, latent.shape[1])
    block_count = (jnp.max(context_lengths) + block_size - 1) // block_size
    initial = (
        jnp.full((row_count, head_count), -1e30, jnp.float32),
        jnp.zeros((row_count, head_count), jnp.float32),
        jnp.zeros((row_count, head_count, VL), jnp.float32),
    )

    def advance(block_index, carried):
        running_max, running_sum, accumulated = carried
        key_block = lax.dynamic_slice_in_dim(latent, block_index * block_size, block_size, 1)
        scores = (
            jnp.einsum("rhc,rkc->rhk", queries, key_block, preferred_element_type=jnp.float32)
            * softmax_scale
        )
        positions = block_index * block_size + jnp.arange(block_size, dtype=jnp.int32)
        included = positions[None, None, :] < context_lengths[:, None, None]
        scores = jnp.where(included, scores, jnp.float32(-1e30))
        new_max = jnp.maximum(running_max, jnp.max(scores, axis=-1))
        factor = jnp.exp(running_max - new_max)
        weights = jnp.where(included, jnp.exp(scores - new_max[:, :, None]), jnp.float32(0.0))
        running_sum = running_sum * factor + jnp.sum(weights, axis=-1)
        product = jnp.einsum(
            "rhk,rkc->rhc",
            weights.astype(jnp.bfloat16),
            key_block[:, :, :VL],
            preferred_element_type=jnp.float32,
        )
        accumulated = accumulated * factor[:, :, None] + product
        return (new_max, running_sum, accumulated)

    final_max, final_sum, accumulated = lax.fori_loop(0, block_count, advance, initial)
    return (accumulated / final_sum[:, :, None]).astype(jnp.bfloat16)


def moved_by(offset, single_row):
    return jax.tree.map(
        lambda part, own: part.astype(own.dtype),
        shifted(for_sending(single_row), "dev", offset),
        single_row,
    )


def send_round(single_row, round_distance, devices):
    branches = [partial(moved_by, offset) for offset in range(1, devices)]
    return lax.switch(round_distance - 1, branches, single_row)


def per_device(
    q_lat, latent_cache, lengths, moves, hidden_in, norm_gain, w_up, w_down, queue_counts, deadline
):
    devices = lax.axis_size("dev")
    my_index = lax.axis_index("dev")
    row_count = latent_cache.shape[0]
    context = latent_cache.shape[1]
    rounds = moves.reshape(MOVE_DEV, devices, 3)
    own_moves = rounds[:, my_index, :]
    leaving = own_moves[:, 0] - my_index * row_count
    distance = (own_moves[:, 2] - my_index) % devices
    own_lengths = lax.dynamic_slice_in_dim(lengths, my_index * row_count, row_count)
    payload = latent_cache[leaving]
    arrivals = []
    for round_index in range(MOVE_DEV):
        arrivals.append(send_round(payload[round_index], distance[round_index], devices))
    travelled = jnp.stack(arrivals, axis=0)
    new_cache = latent_cache.at[leaving].set(travelled[:, :context])
    attn_out = attend(q_lat, latent_cache, own_lengths)
    widened = hidden_in.astype(jnp.float32)
    scaled = lax.rsqrt(jnp.mean(widened * widened, axis=-1, keepdims=True) + 1e-06)
    normed = (widened * scaled * norm_gain.astype(jnp.float32)[None, :]).astype(jnp.bfloat16)
    running = (deadline[:, None] == jnp.arange(BUCKETS, dtype=jnp.int32)[None, :]).astype(
        jnp.float32
    )
    bucket_terms = queue_counts.astype(jnp.float32)[0] + jnp.sum(running, axis=0)
    all_rows = collect(normed, "dev", 0)
    bucket_load = taken_together(bucket_terms, "dev")
    hidden_units = jax.nn.silu(jnp.dot(all_rows, w_up, preferred_element_type=jnp.float32)).astype(
        jnp.bfloat16
    )
    partial_sum = sum_at_owner(
        jnp.dot(hidden_units, w_down, preferred_element_type=jnp.float32), "dev", 0
    )
    mixed = (widened + partial_sum).astype(jnp.bfloat16)
    return (attn_out, new_cache, mixed, bucket_load)


def solution(mesh):
    return jax.shard_map(
        per_device,
        mesh=mesh,
        in_specs=(
            P(("grp", "dev"), None, None),
            P(("grp", "dev"), None, None),
            P("grp"),
            P("grp", None),
            P(("grp", "dev"), None),
            P(),
            P(None, "dev"),
            P("dev", None),
            P(("grp", "dev"), None),
            P(("grp", "dev")),
        ),
        out_specs=(
            P(("grp", "dev"), None, None),
            P(("grp", "dev"), None, None),
            P(("grp", "dev"), None),
            P("grp"),
        ),
        check_vma=False,
    )
```

profile of v0, /device:TPU:42, one launch (start us, length us, event | category | flops | bytes accessed | tf_op | source)
XLA Modules:
  0.0 116.8 jit_solution(6549111723579110028)
XLA Ops:
  0.7 0.7 copy-done.3
  1.6 0.9 broadcast_in_dim.55
  2.5 8.6 %all-to-all-start = ((bf16[16,4,3584]{2,1,0:T(4,128)(2,1)}), bf16[16,4,3584]{2,1,0:T(4,128)(2,1)S(1)}, u32[]{:S(2)}, u32[]{:S(2)}) async-start(bf16[16,4,3584]{2,1,0:T(4,128)(2,1)} %broadcast_in_dim.55), calls=%async_computation | async-start | bytes 917504 | tf_op jit(solution)/shard_map/all_to_all | solution.py:38
  11.1 0.7 fusion.23
  12.6 11.6 %all-to-all-done = bf16[16,4,3584]{2,1,0:T(4,128)(2,1)S(1)} async-done(((bf16[16,4,3584]{2,1,0:T(4,128)(2,1)}), bf16[16,4,3584]{2,1,0:T(4,128)(2,1)S(1)}, u32[]{:S(2)}, u32[]{:S(2)}) %all-to-all-start) | async-done | bytes 458784 | tf_op jit(solution)/shard_map/all_to_all | solution.py:38
  24.2 0.6 broadcast_in_dim.56
  24.8 5.7 %all-to-all-start.2 = ((f32[16,1,8]{2,1,0:T(1,128)}), f32[16,1,8]{2,1,0:T(1,128)S(1)}, u32[]{:S(2)}, u32[]{:S(2)}) async-start(f32[16,1,8]{2,1,0:T(1,128)} %broadcast_in_dim.56), calls=%async_computation.2 | async-start | bytes 16384 | tf_op jit(solution)/shard_map/all_to_all | solution.py:38
  30.6 5.5 %fusion.13 = f32[64,3584]{1,0:T(8,128)S(1)} fusion(bf16[640,3584]{1,0:T(8,128)(2,1)} %param.49, bf16[64,3584]{1,0:T(8,128)(2,1)S(1)} %reshape.84, bf16[3584,640]{1,0:T(8,128)(2,1)} %param.48), kind=kOutput, calls=%fused_computation.57 | convolution fusion | flops 587407360 | bytes 10551296 | tf_op jit(solution)/shard_map/dot_general | solution.py:144
  36.1 1.2 %reshape.85 = f32[16,4,3584]{2,1,0:T(4,128)} reshape(f32[64,3584]{1,0:T(8,128)S(1)} %fusion.13) | data formatting | bytes 1835008 | tf_op jit(solution)/shard_map/reshape | solution.py:51
  37.3 7.4 %all-to-all-start.1 = ((f32[16,4,3584]{2,1,0:T(4,128)}), f32[16,4,3584]{2,1,0:T(4,128)S(1)}, u32[]{:S(2)}, u32[]{:S(2)}) async-start(f32[16,4,3584]{2,1,0:T(4,128)} %reshape.85), calls=%async_computation.1 | async-start | bytes 1835008 | tf_op jit(solution)/shard_map/all_to_all | solution.py:57
  44.7 1.0 while.14
  46.3 0.6 fusion.25
  48.2 1.4 %gather_fusion = bf16[2,256,576]{1,2,0:T(8,128)(2,1)} fusion(bf16[4,256,576]{1,2,0:T(8,128)(2,1)S(1)} %get-tuple-element.296, s32[1024]{0:T(1024)S(1)} %pad_clamp_fusion), kind=kCustom, calls=%fused_computation | custom fusion | bytes 1179656 | tf_op jit(solution)/shard_map/gather | solution.py:124
  49.6 1.4 %copy.85 = bf16[2,256,576]{2,1,0:T(8,128)(2,1)S(1)} copy(bf16[2,256,576]{1,2,0:T(8,128)(2,1)} %gather_fusion) | data formatting | bytes 1179648 | tf_op jit(solution)/shard_map/gather | solution.py:124
  50.9 38.9 %conditional.3 = (bf16[1,256,576]{2,1,0:T(8,128)(2,1)}) conditional(s32[]{:T(128)} %bitcast.63, bf16[2,256,576]{2,1,0:T(8,128)(2,1)S(1)} %copy.85, bf16[2,256,576]{2,1,0:T(8,128)(2,1)S(1)} %copy.85, bf16[2,256,576]{2,1,0:T(8,128)(2,1)S(1)} %copy.85, bf16[2,256,576]{2,1,0:T(8,128)(2,1)S(1)} %copy.85, ...), branch_computations={%region_20.21_spmd, %region_21.22_spmd, %region_22.23_spmd, %regio... | conditional | bytes 1769520 | solution.py:109
  51.0 4.7 %collective-permute-start.24 = (bf16[256,576]{1,0:T(8,128)(2,1)S(1)}, bf16[256,576]{1,0:T(8,128)(2,1)}, u32[]{:S(2)}, u32[]{:S(2)}) collective-permute-start(bf16[256,576]{1,0:T(8,128)(2,1)S(1)} %slice_bitcast_fusion.24), channel_id=1, source_target_pairs={{0,10},{1,11},{2,12},{3,13},{4,14},{5,15},{6,0},{7,1},{8,2},{9,3},... | collective-permute-start | bytes 884744 | tf_op jit(solution)/shard_map/cond/branch_9_fun/ppermute | solution.py:27
  55.7 34.1 %collective-permute-done.24 = bf16[256,576]{1,0:T(8,128)(2,1)} collective-permute-done((bf16[256,576]{1,0:T(8,128)(2,1)S(1)}, bf16[256,576]{1,0:T(8,128)(2,1)}, u32[]{:S(2)}, u32[]{:S(2)}) %collective-permute-start.24) | collective-permute-done | bytes 294944 | tf_op jit(solution)/shard_map/cond/branch_9_fun/ppermute | solution.py:27
  89.8 20.7 %conditional.2 = (bf16[1,256,576]{2,1,0:T(8,128)(2,1)}) conditional(s32[]{:T(128)} %bitcast.62, bf16[2,256,576]{2,1,0:T(8,128)(2,1)S(1)} %copy.85, bf16[2,256,576]{2,1,0:T(8,128)(2,1)S(1)} %copy.85, bf16[2,256,576]{2,1,0:T(8,128)(2,1)S(1)} %copy.85, bf16[2,256,576]{2,1,0:T(8,128)(2,1)S(1)} %copy.85, ...), branch_computations={%region_5.6_spmd, %region_6.7_spmd, %region_7.8_spmd, %region_8.9_... | conditional | bytes 1769520 | solution.py:109
  89.9 20.5 %collective-permute-done.7 = bf16[256,576]{1,0:T(8,128)(2,1)} collective-permute-done((bf16[256,576]{1,0:T(8,128)(2,1)S(1)}, bf16[256,576]{1,0:T(8,128)(2,1)}, u32[]{:S(2)}, u32[]{:S(2)}) %collective-permute-start.7) | collective-permute-done | bytes 294944 | tf_op jit(solution)/shard_map/cond/branch_7_fun/ppermute | solution.py:27
  110.5 2.0 %pad_maximum_fusion = bf16[2,256,576]{2,1,0:T(8,128)(2,1)} fusion(bf16[1,256,576]{2,1,0:T(8,128)(2,1)} %get-tuple-element.295, bf16[1,256,576]{2,1,0:T(8,128)(2,1)} %get-tuple-element.294), kind=kLoop, calls=%fused_computation.51 | loop fusion | flops 294912 | bytes 1179648 | tf_op jit(solution)/shard_map/stack | solution.py:128
  112.5 1.3 %copy.115 = bf16[2,256,576]{1,2,0:T(8,128)(2,1)S(1)} copy(bf16[2,256,576]{2,1,0:T(8,128)(2,1)} %pad_maximum_fusion) | data formatting | bytes 1179648 | tf_op jit(solution)/shard_map/stack | solution.py:128
  113.8 0.8 scatter_fusion
  114.6 0.9 divide_convert_fusion
  116.2 0.6 fusion.18
  (48 shorter events, 2.8 us)
Async XLA Ops:
  0.6 0.7 copy-start.3
  0.6 0.9 copy-start.4
  1.4 9.7 %copy-start.6 = (s32[64]{0:T(128)S(1)}, s32[64]{0:T(128)}, u32[]{:S(2)}) copy-start(s32[64]{0:T(128)} %param.44) | copy-start | bytes 772
  1.4 11.1 %copy-start.7 = (s32[4]{0:T(128)S(1)}, s32[4]{0:T(128)}, u32[]{:S(2)}) copy-start(s32[4]{0:T(128)} %param.51) | copy-start | bytes 52
  1.4 11.2 %copy-start.8 = (s32[1,8]{1,0:T(1,128)S(1)}, s32[1,8]{1,0:T(1,128)}, u32[]{:S(2)}) copy-start(s32[1,8]{1,0:T(1,128)} %param.50) | copy-start | bytes 100
  2.5 21.6 %all-to-all-start = ((bf16[16,4,3584]{2,1,0:T(4,128)(2,1)}), bf16[16,4,3584]{2,1,0:T(4,128)(2,1)S(1)}, u32[]{:S(2)}, u32[]{:S(2)}) async-start(bf16[16,4,3584]{2,1,0:T(4,128)(2,1)} %broadcast_in_dim.55), calls=%async_computation | async-start | bytes 917504 | tf_op jit(solution)/shard_map/all_to_all | solution.py:38
  24.8 12.5 %all-to-all-start.2 = ((f32[16,1,8]{2,1,0:T(1,128)}), f32[16,1,8]{2,1,0:T(1,128)S(1)}, u32[]{:S(2)}, u32[]{:S(2)}) async-start(f32[16,1,8]{2,1,0:T(1,128)} %broadcast_in_dim.56), calls=%async_computation.2 | async-start | bytes 16384 | tf_op jit(solution)/shard_map/all_to_all | solution.py:38
  37.3 7.4 %copy-start.1 = (bf16[4,256,576]{1,2,0:T(8,128)(2,1)S(1)}, bf16[4,256,576]{1,2,0:T(8,128)(2,1)}, u32[]{:S(2)}) copy-start(bf16[4,256,576]{1,2,0:T(8,128)(2,1)} %param.43) | copy-start | bytes 3538948
  37.3 7.4 %copy-start.2 = (bf16[4,64,576]{2,1,0:T(8,128)(2,1)S(1)}, bf16[4,64,576]{2,1,0:T(8,128)(2,1)}, u32[]{:S(2)}) copy-start(bf16[4,64,576]{2,1,0:T(8,128)(2,1)} %param.42) | copy-start | bytes 884740
  37.3 78.8 %all-to-all-start.1 = ((f32[16,4,3584]{2,1,0:T(4,128)}), f32[16,4,3584]{2,1,0:T(4,128)S(1)}, u32[]{:S(2)}, u32[]{:S(2)}) async-start(f32[16,4,3584]{2,1,0:T(4,128)} %reshape.85), calls=%async_computation.1 | async-start | bytes 1835008 | tf_op jit(solution)/shard_map/all_to_all | solution.py:57
  44.7 1.1 copy-start.5
  51.0 38.8 %collective-permute-start.24 = (bf16[256,576]{1,0:T(8,128)(2,1)S(1)}, bf16[256,576]{1,0:T(8,128)(2,1)}, u32[]{:S(2)}, u32[]{:S(2)}) collective-permute-start(bf16[256,576]{1,0:T(8,128)(2,1)S(1)} %slice_bitcast_fusion.24), channel_id=1, source_target_pairs={{0,10},{1,11},{2,12},{3,13},{4,14},{5,15},{6,0},{7,1},{8,2},{9,3},... | collective-permute-start | bytes 884744 | tf_op jit(solution)/shard_map/cond/branch_9_fun/ppermute | solution.py:27
  89.8 20.6 %collective-permute-start.7 = (bf16[256,576]{1,0:T(8,128)(2,1)S(1)}, bf16[256,576]{1,0:T(8,128)(2,1)}, u32[]{:S(2)}, u32[]{:S(2)}) collective-permute-start(bf16[256,576]{1,0:T(8,128)(2,1)S(1)} %slice_bitcast_fusion.7), channel_id=1, source_target_pairs={{0,8},{1,9},{2,10},{3,11},{4,12},{5,13},{6,14},{7,15},{8,0},{9,1},... | collective-permute-start | bytes 884744 | tf_op jit(solution)/shard_map/cond/branch_7_fun/ppermute | solution.py:27
  114.6 2.3 %copy-start = (bf16[4,256,576]{1,2,0:T(8,128)(2,1)}, bf16[4,256,576]{1,2,0:T(8,128)(2,1)S(1)}, u32[]{:S(2)}) copy-start(bf16[4,256,576]{1,2,0:T(8,128)(2,1)S(1)} %scatter_fusion) | copy-start | bytes 3538948
where the time goes:
time: 117 us
  waiting for transfers between devices  66.2 us (57%)
  starting transfers between devices  26.5 us (23%)
  local copies, waits for them, and re-layouts  9.37 us (8%)
  matrix products  6.14 us (5%)
  other arithmetic  5.78 us (5%)
  between operations  2.77 us (2%)
    ppermute x2, waiting for transfers between devices, shifted(): return lax.ppermute(value, axis, pairs)  54.6 us
    all_to_all x2, starting transfers between devices, sent_to_all(): lax.all_to_all(jnp.broadcast_to(x[None], (peers, *x.shape)), axis, 0, 0,...  14.3 us
    all_to_all x2, waiting for transfers between devices, sent_to_all(): lax.all_to_all(jnp.broadcast_to(x[None], (peers, *x.shape)), axis, 0, 0,...  11.6 us
    all_to_all x1, starting transfers between devices, sum_at_owner(): lax.all_to_all(tiles, axis, split_axis=0, concat_axis=0, tiled=True)  7.35 us
    dot_general x1, matrix products, per_device(): jnp.dot(hidden_units, w_down, preferred_element_type=jnp.float32)  5.45 us
    ppermute x2, starting transfers between devices, shifted(): return lax.ppermute(value, axis, pairs)  4.79 us
    gather x2, local copies, waits for them, and re-layouts, per_device(): payload = latent_cache[leaving]  2.76 us
  transfers between devices with their start and end apart: 5, of which 3 were waited for; matrix products, arithmetic and copies ran while one was open for 15% of the time, Pallas kernels for 0%

commit v1 on v0

v1 whole, which is shorter than its diff:
```python
from functools import partial

import jax
import jax.numpy as jnp
from jax import lax
from jax.experimental import pallas as pl
from jax.experimental.pallas import tpu as pltpu
from jax.sharding import PartitionSpec as P


VL = 512
CONTEXT = 256
BUCKETS = 8
LANES = 128
MIB = 1 << 20

softmax_scale = 192.0 ** (-0.5)

VMEM = pltpu.VMEM
SMEM = pltpu.SMEM
HBM = pltpu.HBM


def whole(space):
    return pl.BlockSpec(memory_space=space)


def shifted(value, axis, steps):
    count = lax.axis_size(axis)
    pairs = [(source, (source + steps) % count) for source in range(count)]
    return lax.ppermute(value, axis, pairs)


def piece_windows(count, depth, lanes):
    across = CONTEXT // lanes
    down = count // across
    return [
        (pl.ds((i % down) * depth, depth), pl.ds((i // down) * lanes, lanes))
        for i in range(count)
    ]


def prepare_kernel(
    devices, moves_ref, cache_ref, hidden_ref, gain_ref, queue_ref, deadline_ref,
    half_ref, pieces_ref, rows_ref, info_ref, sems,
):
    me = lax.axis_index("dev")
    own_rows = cache_ref.shape[0]
    leaving = [moves_ref[0, j * devices + me] - me * own_rows for j in range(2)]
    distance = [
        (moves_ref[2, j * devices + me] - me + devices) % devices for j in range(2)
    ]
    first_is_half = distance[0] == devices // 2
    half_row = jnp.where(first_is_half, leaving[0], leaving[1])
    other_row = jnp.where(first_is_half, leaving[1], leaving[0])
    info_ref[0] = jnp.where(first_is_half, distance[1], distance[0])
    info_ref[1] = half_row
    info_ref[2] = other_row
    copies = [
        pltpu.make_async_copy(cache_ref.at[half_row], half_ref, sems.at[0]),
    ] + [
        pltpu.make_async_copy(
            cache_ref.at[other_row, rows, lanes], pieces_ref.at[i], sems.at[1 + i]
        )
        for i, (rows, lanes) in enumerate(piece_windows(*pieces_ref.shape))
    ]
    for copy in copies:
        copy.start()
    features = hidden_ref.shape[1]
    wide = hidden_ref[...].astype(jnp.float32)
    scaled = lax.rsqrt(jnp.mean(wide * wide, axis=-1, keepdims=True) + 1e-06)
    normed = wide * scaled * gain_ref[...].astype(jnp.float32)[None, :]
    block_rows = 2 * own_rows
    place = lax.broadcasted_iota(jnp.int32, (block_rows, features), 0) // own_rows
    doubled = jnp.concatenate([normed, normed], axis=0)
    rows_ref[:, 0:features] = jnp.where(place == me % 2, doubled, 0.0).astype(jnp.bfloat16)
    extra = rows_ref.shape[1] - features
    lane = lax.broadcasted_iota(jnp.int32, (block_rows, extra), 1)
    row = lax.broadcasted_iota(jnp.int32, (block_rows, extra), 0)
    counts = jnp.zeros((block_rows, extra), jnp.int32)
    for b in range(BUCKETS):
        count = queue_ref[0, b]
        for r in range(own_rows):
            count = count + (deadline_ref[r] == b).astype(jnp.int32)
        counts = jnp.where(lane == b, count, counts)
    counts = jnp.where(row == (me % 2) * own_rows, counts, 0)
    rows_ref[:, features:] = counts.astype(jnp.float32).astype(jnp.bfloat16)
    for copy in copies:
        copy.wait()


def prepare(moves, cache, hidden_in, norm_gain, queue_counts, deadline):
    devices = lax.axis_size("dev")
    own_rows, depth, context = cache.shape
    features = hidden_in.shape[1]
    return pl.pallas_call(
        partial(prepare_kernel, devices),
        out_shape=(
            jax.ShapeDtypeStruct((depth, context), cache.dtype),
            jax.ShapeDtypeStruct(
                (devices, depth * context // (devices * LANES), LANES), cache.dtype
            ),
            jax.ShapeDtypeStruct((2 * own_rows, features + 2 * LANES), jnp.bfloat16),
            jax.ShapeDtypeStruct((3,), jnp.int32),
        ),
        in_specs=[
            whole(SMEM), whole(HBM), whole(VMEM), whole(VMEM), whole(SMEM), whole(SMEM),
        ],
        out_specs=(whole(VMEM), whole(VMEM), whole(VMEM), whole(SMEM)),
        scratch_shapes=[pltpu.SemaphoreType.DMA((devices + 1,))],
        name="prepare",
    )(moves, cache, hidden_in, norm_gain, queue_counts, deadline)


def attend_kernel(lengths_ref, queries_ref, cache_ref, out_ref, kept_ref):
    own_rows = pl.num_programs(0)
    row = pl.program_id(0)
    length = lengths_ref[lax.axis_index("dev") * own_rows + row]
    latent = cache_ref[0]
    kept_ref[0] = latent
    scores = (
        jnp.dot(queries_ref[0], latent, preferred_element_type=jnp.float32) * softmax_scale
    )
    included = lax.broadcasted_iota(jnp.int32, scores.shape, 1) < length
    scores = jnp.where(included, scores, jnp.float32(-1e30))
    largest = jnp.max(scores, axis=-1, keepdims=True)
    weights = jnp.where(included, jnp.exp(scores - largest), jnp.float32(0.0))
    total = jnp.sum(weights, axis=-1, keepdims=True)
    summed = lax.dot_general(
        weights.astype(jnp.bfloat16),
        latent[0:VL, :],
        (((1,), (1,)), ((), ())),
        preferred_element_type=jnp.float32,
    )
    out_ref[0] = (summed / total).astype(jnp.bfloat16)


def attend(lengths, queries, cache):
    own_rows, heads, depth = queries.shape
    context = cache.shape[2]
    block = lambda *dims: pl.BlockSpec((1, *dims), lambda r: (r, 0, 0))
    return pl.pallas_call(
        attend_kernel,
        grid=(own_rows,),
        out_shape=(
            jax.ShapeDtypeStruct((own_rows, heads, VL), jnp.bfloat16),
            jax.ShapeDtypeStruct(cache.shape, cache.dtype),
        ),
        in_specs=[whole(SMEM), block(heads, depth), block(depth, context)],
        out_specs=(block(heads, VL), block(depth, context)),
        compiler_params=pltpu.CompilerParams(vmem_limit_bytes=12 * MIB),
        name="attend",
    )(lengths, queries, cache)


def feed_kernel(
    own_ref, near_ref, next_ref, far_ref, other_near_ref, other_next_ref, other_far_ref,
    up_ref, down_ref,
    own_out, give_out, keep_out, give_far_out, keep_far_out, load_ref,
    rows_buf, up_buf, down_buf, up_sems, down_sems,
):
    pieces, depth, _ = up_buf.shape
    columns = down_buf.shape[2]
    up_copies = [
        pltpu.make_async_copy(
            up_ref.at[pl.ds(i * depth, depth), :], up_buf.at[i], up_sems.at[i]
        )
        for i in range(pieces)
    ]
    down_copies = [
        pltpu.make_async_copy(
            down_ref.at[:, pl.ds(i * columns, columns)], down_buf.at[i], down_sems.at[i]
        )
        for i in range(down_buf.shape[0])
    ]
    for copy in up_copies + down_copies:
        copy.start()
    first_core = lax.axis_index("dev") % 2 == 0
    block = own_ref.shape[0]
    width = own_ref.shape[1]
    for at, part in (
        (0, own_ref), (1, near_ref), (2, next_ref), (4, other_near_ref), (5, other_next_ref),
    ):
        rows_buf[at * block : at * block + part.shape[0], :] = part[...]
    far = far_ref[...]
    other_far = other_far_ref[...]
    rows_buf[7 * block :, 0 : width // 2] = jnp.where(first_core, far, other_far)
    rows_buf[7 * block :, width // 2 :] = jnp.where(first_core, other_far, far)
    features = pieces * depth
    counts = rows_buf[:, features : features + LANES].astype(jnp.float32)
    load_ref[...] = jnp.sum(counts, axis=0)[0:BUCKETS]
    up = None
    for i in range(pieces):
        up_copies[i].wait()
        term = jnp.dot(
            rows_buf[:, i * depth : (i + 1) * depth],
            up_buf[i],
            preferred_element_type=jnp.float32,
        )
        up = term if up is None else up + term
    hidden = (up / (1.0 + jnp.exp(-up))).astype(jnp.bfloat16)
    half = features // 2
    for i, copy in enumerate(down_copies):
        copy.wait()
        product = jnp.dot(hidden, down_buf[i], preferred_element_type=jnp.float32)
        at = slice(i * columns, (i + 1) * columns)
        own_out[:, at] = product[0:block]
        give_out[:, at] = product[block : 4 * block]
        keep_out[:, at] = product[4 * block : 7 * block]
        far_sums = product[7 * block :]
        for low, high in ((0, half), (half, features)):
            start, stop = max(low, i * columns), min(high, (i + 1) * columns)
            if start < stop:
                piece = far_sums[:, start - i * columns : stop - i * columns]
                target = slice(start - low, stop - low)
                mine = first_core if low == 0 else jnp.logical_not(first_core)

                @pl.when(mine)
                def _(piece=piece, target=target):
                    keep_far_out[:, target] = piece

                @pl.when(jnp.logical_not(mine))
                def _(piece=piece, target=target):
                    give_far_out[:, target] = piece


def feed(parts, w_up, w_down):
    features, units = w_up.shape
    pieces = 7
    depth = features // pieces
    block, width = parts[0].shape
    wide = lambda rows, columns: jax.ShapeDtypeStruct((rows, columns), jnp.float32)
    return pl.pallas_call(
        feed_kernel,
        out_shape=(
            wide(block, features),
            wide(3 * block, features),
            wide(3 * block, features),
            wide(block, features // 2),
            wide(block, features // 2),
            jax.ShapeDtypeStruct((BUCKETS,), jnp.float32),
        ),
        in_specs=[whole(VMEM)] * 7 + [whole(HBM)] * 2,
        out_specs=(whole(VMEM),) * 6,
        scratch_shapes=[
            pltpu.VMEM((8 * block, width), jnp.bfloat16),
            pltpu.VMEM((pieces, depth, units), w_up.dtype),
            pltpu.VMEM((pieces, units, depth), w_down.dtype),
            pltpu.SemaphoreType.DMA((pieces,)),
            pltpu.SemaphoreType.DMA((pieces,)),
        ],
        compiler_params=pltpu.CompilerParams(vmem_limit_bytes=20 * MIB),
        name="feed",
    )(*parts, w_up, w_down)


def turn_kernel(devices, info_ref, pieces_ref, out_ref):
    steps = info_ref[0]
    for d in range(devices):
        out_ref[d] = pieces_ref[(d - steps + devices) % devices]


def turn(info, pieces):
    return pl.pallas_call(
        partial(turn_kernel, pieces.shape[0]),
        out_shape=jax.ShapeDtypeStruct(pieces.shape, pieces.dtype),
        in_specs=[whole(SMEM), whole(VMEM)],
        out_specs=whole(VMEM),
        compiler_params=pltpu.CompilerParams(vmem_limit_bytes=4 * MIB),
        name="turn",
    )(info, pieces)


def patch_half_kernel(info_ref, half_ref, kept_ref, out_ref, sem):
    copy = pltpu.make_async_copy(half_ref, out_ref.at[info_ref[1]], sem)
    copy.start()
    copy.wait()


def patch_half(info, half, kept):
    return pl.pallas_call(
        patch_half_kernel,
        out_shape=jax.ShapeDtypeStruct(kept.shape, kept.dtype),
        in_specs=[whole(SMEM), whole(VMEM), whole(pl.ANY)],
        out_specs=whole(pl.ANY),
        input_output_aliases={2: 0},
        scratch_shapes=[pltpu.SemaphoreType.DMA],
        compiler_params=pltpu.CompilerParams(vmem_limit_bytes=4 * MIB),
        name="patch_half",
    )(info, half, kept)


def patch_pieces_kernel(info_ref, pieces_ref, kept_ref, out_ref, sems):
    copies = [
        pltpu.make_async_copy(
            pieces_ref.at[i], out_ref.at[info_ref[2], rows, lanes], sems.at[i]
        )
        for i, (rows, lanes) in enumerate(piece_windows(*pieces_ref.shape))
    ]
    for copy in copies:
        copy.start()
    for copy in copies:
        copy.wait()


def patch_pieces(info, pieces, kept):
    return pl.pallas_call(
        patch_pieces_kernel,
        out_shape=jax.ShapeDtypeStruct(kept.shape, kept.dtype),
        in_specs=[whole(SMEM), whole(VMEM), whole(pl.ANY)],
        out_specs=whole(pl.ANY),
        input_output_aliases={2: 0},
        scratch_shapes=[pltpu.SemaphoreType.DMA((pieces.shape[0],))],
        compiler_params=pltpu.CompilerParams(vmem_limit_bytes=4 * MIB),
        name="patch_pieces",
    )(info, pieces, kept)


def exchange(value):
    return lax.all_to_all(value, "dev", 0, 0, tiled=True)


def swapped(value):
    count = lax.axis_size("dev")
    return lax.ppermute(value, "dev", [(s, s ^ 1) for s in range(count)])


def outward(value, chips):
    count = lax.axis_size("dev")
    pairs = [(s, (s + (2 * chips if s % 2 == 0 else -2 * chips)) % count) for s in range(count)]
    return lax.ppermute(value, "dev", pairs)


SHRINK = 0.25


def narrow(x):
    return (x * SHRINK).astype(jnp.float16)


def widen(x):
    return x.astype(jnp.float32) * (1.0 / SHRINK)


def per_device(
    q_lat, latent_cache, lengths, moves, hidden_in, norm_gain, w_up, w_down, queue_counts, deadline
):
    devices = lax.axis_size("dev")
    own_rows, _ = hidden_in.shape
    first_core = lax.axis_index("dev") % 2 == 0
    block = 2 * own_rows
    cache = jnp.swapaxes(latent_cache, 1, 2)
    half, pieces, rows, info = prepare(
        moves.T, cache, hidden_in, norm_gain, queue_counts, deadline
    )
    own = rows + swapped(rows)
    width = own.shape[1] // 2
    far = outward(jnp.where(first_core, own[:, :width], own[:, width:]), 4)
    near = outward(own, 1)
    pieces = exchange(pieces)
    nxt = outward(jnp.concatenate([own, near], axis=0), 2)
    half = shifted(half, "dev", devices // 2)
    attn_out, kept = attend(lengths, q_lat, cache)
    other_near = swapped(near)
    other_far = swapped(far)
    other_next = swapped(nxt)
    own_sums, give, keep, give_far, keep_far, load = feed(
        (own, near, nxt, far, other_near, other_next, other_far), w_up, w_down
    )
    pieces = turn(info, pieces)
    got_far = swapped(give_far)
    got = swapped(give)
    sums_far = outward(narrow(keep_far + got_far), 4)
    sums_next = outward(narrow(keep[block:] + got[block:]), 2)
    pieces = exchange(pieces)
    kept = patch_half(info, half, kept)
    near_sums = keep[:block] + got[:block] + widen(sums_next[block:])
    sums_near = outward(narrow(near_sums), 1)
    wide_far = widen(sums_far)
    zeros = jnp.zeros_like(wide_far)
    both = jnp.concatenate(
        [jnp.where(first_core, wide_far, zeros), jnp.where(first_core, zeros, wide_far)],
        axis=1,
    )
    total = own_sums + widen(sums_next[:block]) + widen(sums_near) + both
    low, high = total[:own_rows], total[own_rows:]
    got_total = swapped(jnp.where(first_core, high, low))
    summed = jnp.where(first_core, low, high) + got_total
    mixed = (hidden_in.astype(jnp.float32) + summed).astype(jnp.bfloat16)
    kept = patch_pieces(info, pieces, kept)
    return attn_out, jnp.swapaxes(kept, 1, 2), mixed, load


def solution(mesh):
    return jax.shard_map(
        per_device,
        mesh=mesh,
        in_specs=(
            P(("grp", "dev"), None, None),
            P(("grp", "dev"), None, None),
            P("grp"),
            P("grp", None),
            P(("grp", "dev"), None),
            P(),
            P(None, "dev"),
            P("dev", None),
            P(("grp", "dev"), None),
            P(("grp", "dev")),
        ),
        out_specs=(
            P(("grp", "dev"), None, None),
            P(("grp", "dev"), None, None),
            P(("grp", "dev"), None),
            P("grp"),
        ),
        check_vma=False,
    )
```

time: 117 us -> 105 us (0.90)
  the two profiles are of different devices: /device:TPU:42 before, /device:TPU:1 now
where the time goes in v1:
time: 105 us
  starting transfers between devices  55.2 us (53%)
  waiting for transfers between devices  26.9 us (26%)
  Pallas kernels  15.9 us (15%)
  local copies, waits for them, and re-layouts  4.63 us (4%)
  other arithmetic  1.67 us (2%)
    ppermute x6, starting transfers between devices, outward(): return lax.ppermute(value, 'dev', pairs)  26.3 us
    ppermute x7, starting transfers between devices, swapped(): return lax.ppermute(value, 'dev', [(s, s ^ 1) for s in range(count)])  14.3 us
    ppermute x6, waiting for transfers between devices, outward(): return lax.ppermute(value, 'dev', pairs)  12.8 us
    all_to_all x2, waiting for transfers between devices, exchange(): return lax.all_to_all(value, 'dev', 0, 0, tiled=True)  11.6 us
    all_to_all x2, starting transfers between devices, exchange(): return lax.all_to_all(value, 'dev', 0, 0, tiled=True)  9.23 us
    pallas_call x1, Pallas kernels, feed(): pl.pallas_call(feed_kernel, out_shape=(wide(block, features), wide(3 * bl...  5.68 us
    ppermute x1, starting transfers between devices, shifted(): return lax.ppermute(value, axis, pairs)  5.35 us
    unnamed x16, local copies, waits for them, and re-layouts  4.63 us
  transfers between devices with their start and end apart: 16, of which 9 were waited for; matrix products, arithmetic and copies ran while one was open for 1% of the time, Pallas kernels for 6%

profile of v1, /device:TPU:1, one launch (start us, length us, event | category | flops | bytes accessed | tf_op | source)
XLA Modules:
  0.0 105.0 jit_solution(15923548817092030146)
XLA Ops:
  0.6 2.9 %prepare.1 = (bf16[576,256]{1,0:T(8,128)(2,1)}, bf16[16,72,128]{2,1,0:T(8,128)(2,1)}, bf16[8,3840]{1,0:T(8,128)(2,1)}, s32[3]{0:T(128)}) custom-call(s32[3,32]{1,0:T(4,128)} %bitcast.6, bf16[4,576,256]{2,1,0:T(8,128)(2,1)} %bitcast.3, bf16[4,3584]{1,0:T(4,128)(2,1)} %hidden_ref.1, bf16[3584]{0:T(1024)(128)(2,1)} %gain_ref.1, s32[1,8]{1,0:T(1,128)} %queue_ref.1, ...), custom_call_target="tpu_custom_call" | custom-call | tf_op jit(solution)/shard_map/prepare/pallas_call | solution.py:96
  3.5 3.3 %collective-permute-start.1 = (bf16[8,3840]{1,0:T(8,128)(2,1)}, bf16[8,3840]{1,0:T(8,128)(2,1)S(1)}, u32[]{:S(2)}, u32[]{:S(2)}) collective-permute-start(bf16[8,3840]{1,0:T(8,128)(2,1)} %get-tuple-element.21), channel_id=1, source_target_pairs={{0,1},{1,0},{2,3},{3,2},{4,5},{5,4},{6,7},{7,6},{8,9},{9,8},{10,11... | collective-permute-start | bytes 184328 | tf_op jit(solution)/shard_map/ppermute | solution.py:325
  8.7 3.9 %collective-permute-start.2 = (bf16[8,3840]{1,0:T(8,128)(2,1)S(1)}, bf16[8,3840]{1,0:T(8,128)(2,1)S(1)}, u32[]{:S(2)}, u32[]{:S(2)}) collective-permute-start(bf16[8,3840]{1,0:T(8,128)(2,1)S(1)} %add.35.own_ref), channel_id=1, source_target_pairs={{0,2},{1,15},{2,4},{3,1},{4,6},{5,3},{6,8},{7,5},{8,10},{9,7},{10,... | collective-permute-start | bytes 184328 | tf_op jit(solution)/shard_map/ppermute | solution.py:331
  12.7 1.3 %collective-permute-done.2.near_ref = bf16[8,3840]{1,0:T(8,128)(2,1)S(1)} collective-permute-done((bf16[8,3840]{1,0:T(8,128)(2,1)S(1)}, bf16[8,3840]{1,0:T(8,128)(2,1)S(1)}, u32[]{:S(2)}, u32[]{:S(2)}) %collective-permute-start.2) | collective-permute-done | bytes 61472 | tf_op jit(solution)/shard_map/ppermute | solution.py:331
  14.0 2.3 %collective-permute-start.3 = (bf16[16,3840]{1,0:T(8,128)(2,1)S(1)}, bf16[16,3840]{1,0:T(8,128)(2,1)S(1)}, u32[]{:S(2)}, u32[]{:S(2)}) collective-permute-start(bf16[16,3840]{1,0:T(8,128)(2,1)S(1)} %pad_maximum_fusion), channel_id=1, source_target_pairs={{0,4},{1,13},{2,6},{3,15},{4,8},{5,1},{6,10},{7,3},{8,12},{9,5},{1... | collective-permute-start | bytes 368648 | tf_op jit(solution)/shard_map/ppermute | solution.py:331
  16.3 3.3 %collective-permute-done.3.next_ref = bf16[16,3840]{1,0:T(8,128)(2,1)S(1)} collective-permute-done((bf16[16,3840]{1,0:T(8,128)(2,1)S(1)}, bf16[16,3840]{1,0:T(8,128)(2,1)S(1)}, u32[]{:S(2)}, u32[]{:S(2)}) %collective-permute-start.3) | collective-permute-done | bytes 122912 | tf_op jit(solution)/shard_map/ppermute | solution.py:331
  19.6 3.6 %collective-permute-start.6 = (bf16[16,3840]{1,0:T(8,128)(2,1)S(1)}, bf16[16,3840]{1,0:T(8,128)(2,1)S(1)}, u32[]{:S(2)}, u32[]{:S(2)}) collective-permute-start(bf16[16,3840]{1,0:T(8,128)(2,1)S(1)} %collective-permute-done.3.next_ref), channel_id=1, source_target_pairs={{0,1},{1,0},{2,3},{3,2},{4,5},{5,4},{6,7},{7,6},{8,9},{9,8},{10,11... | collective-permute-start | bytes 368648 | tf_op jit(solution)/shard_map/ppermute | solution.py:325
  23.2 3.7 %collective-permute-start.4 = (bf16[8,1920]{1,0:T(8,128)(2,1)S(1)}, bf16[8,1920]{1,0:T(8,128)(2,1)S(1)}, u32[]{:S(2)}, u32[]{:S(2)}) collective-permute-start(bf16[8,1920]{1,0:T(8,128)(2,1)S(1)} %slice_select_fusion.1), channel_id=1, source_target_pairs={{0,8},{1,9},{2,10},{3,11},{4,12},{5,13},{6,14},{7,15},{8,0},{9,1},... | collective-permute-start | bytes 92168 | tf_op jit(solution)/shard_map/ppermute | solution.py:331
  27.3 2.6 %collective-permute-done.4.far_ref = bf16[8,1920]{1,0:T(8,128)(2,1)S(1)} collective-permute-done((bf16[8,1920]{1,0:T(8,128)(2,1)S(1)}, bf16[8,1920]{1,0:T(8,128)(2,1)S(1)}, u32[]{:S(2)}, u32[]{:S(2)}) %collective-permute-start.4) | collective-permute-done | bytes 30752 | tf_op jit(solution)/shard_map/ppermute | solution.py:331
  29.8 1.7 %collective-permute-start.7 = (bf16[8,1920]{1,0:T(8,128)(2,1)S(1)}, bf16[8,1920]{1,0:T(8,128)(2,1)S(1)}, u32[]{:S(2)}, u32[]{:S(2)}) collective-permute-start(bf16[8,1920]{1,0:T(8,128)(2,1)S(1)} %collective-permute-done.4.far_ref), channel_id=1, source_target_pairs={{0,1},{1,0},{2,3},{3,2},{4,5},{5,4},{6,7},{7,6},{8,9},{9,8},{10,11... | collective-permute-start | bytes 92168 | tf_op jit(solution)/shard_map/ppermute | solution.py:325
  32.4 2.3 %copy-done.1 = bf16[3584,640]{1,0:T(8,128)(2,1)S(1)} copy-done((bf16[3584,640]{1,0:T(8,128)(2,1)S(1)}, bf16[3584,640]{1,0:T(8,128)(2,1)}, u32[]{:S(2)}) %copy-start.1) | copy-done | bytes 4587544
  34.7 2.3 %copy-done.2 = bf16[640,3584]{1,0:T(8,128)(2,1)S(1)} copy-done((bf16[640,3584]{1,0:T(8,128)(2,1)S(1)}, bf16[640,3584]{1,0:T(8,128)(2,1)}, u32[]{:S(2)}) %copy-start.2) | copy-done | bytes 4587544
  37.0 5.7 %feed.1 = (f32[8,3584]{1,0:T(8,128)S(1)}, f32[24,3584]{1,0:T(8,128)S(1)}, f32[24,3584]{1,0:T(8,128)S(1)}, f32[8,1792]{1,0:T(8,128)S(1)}, f32[8,1792]{1,0:T(8,128)S(1)}, /*index=5*/f32[8]{0:T(128)}) custom-call(bf16[8,3840]{1,0:T(8,128)(2,1)S(1)} %add.35.own_ref, bf16[8,3840]{1,0:T(8,128)(2,1)S(1)} %collective-permute-done.2.near_ref, ...), custom_call_target="tpu_custom_call" | custom-call | tf_op jit(solution)/shard_map/feed/pallas_call | solution.py:233
  43.1 5.2 %all-to-all-start = ((bf16[16,72,128]{2,1,0:T(8,128)(2,1)}), bf16[16,72,128]{2,1,0:T(8,128)(2,1)S(1)}, u32[]{:S(2)}, u32[]{:S(2)}) async-start(bf16[16,72,128]{2,1,0:T(8,128)(2,1)} %get-tuple-element.18), calls=%async_computation | async-start | bytes 589824 | tf_op jit(solution)/shard_map/all_to_all | solution.py:320
  48.3 5.3 %collective-permute-start = (bf16[576,256]{1,0:T(8,128)(2,1)S(1)}, bf16[576,256]{1,0:T(8,128)(2,1)S(1)}, u32[]{:S(2)}, u32[]{:S(2)}) collective-permute-start(bf16[576,256]{1,0:T(8,128)(2,1)S(1)} %copy-done.7), channel_id=1, source_target_pairs={{0,8},{1,9},{2,10},{3,11},{4,12},{5,13},{6,14},{7,15},{8,0},{9,1},... | collective-permute-start | bytes 884744 | tf_op jit(solution)/shard_map/ppermute | solution.py:31
  55.2 2.9 %collective-permute-start.12 = (f16[8,1792]{1,0:T(8,128)(2,1)S(1)}, f16[8,1792]{1,0:T(8,128)(2,1)S(1)}, u32[]{:S(2)}, u32[]{:S(2)}) collective-permute-start(f16[8,1792]{1,0:T(8,128)(2,1)S(1)} %multiply_convert_fusion), channel_id=1, source_target_pairs={{0,8},{1,9},{2,10},{3,11},{4,12},{5,13},{6,14},{7,15},{8,0},{9,1},... | collective-permute-start | bytes 86024 | tf_op jit(solution)/shard_map/ppermute | solution.py:331
  58.1 4.4 %collective-permute-done.9 = f16[16,3584]{1,0:T(8,128)(2,1)S(1)} collective-permute-done((f16[16,3584]{1,0:T(8,128)(2,1)S(1)}, f16[16,3584]{1,0:T(8,128)(2,1)S(1)}, u32[]{:S(2)}, u32[]{:S(2)}) %collective-permute-start.9) | collective-permute-done | bytes 114720 | tf_op jit(solution)/shard_map/ppermute | solution.py:331
  62.6 13.1 %collective-permute-start.10 = (f16[8,3584]{1,0:T(8,128)(2,1)S(1)}, f16[8,3584]{1,0:T(8,128)(2,1)S(1)}, u32[]{:S(2)}, u32[]{:S(2)}) collective-permute-start(f16[8,3584]{1,0:T(8,128)(2,1)S(1)} %fusion.4), channel_id=1, source_target_pairs={{0,2},{1,15},{2,4},{3,1},{4,6},{5,3},{6,8},{7,5},{8,10},{9,7},{10,... | collective-permute-start | bytes 172040 | tf_op jit(solution)/shard_map/ppermute | solution.py:331
  76.9 4.3 %collective-permute-start.13 = (f32[4,3584]{1,0:T(4,128)S(1)}, f32[4,3584]{1,0:T(4,128)S(1)}, u32[]{:S(2)}, u32[]{:S(2)}) collective-permute-start(f32[4,3584]{1,0:T(4,128)S(1)} %slice_select_fusion), channel_id=1, source_target_pairs={{0,1},{1,0},{2,3},{3,2},{4,5},{5,4},{6,7},{7,6},{8,9},{9,8},{10,11... | collective-permute-start | bytes 172040 | tf_op jit(solution)/shard_map/ppermute | solution.py:325
  81.3 3.4 %attend.1 = (bf16[4,64,512]{2,1,0:T(8,128)(2,1)}, bf16[4,576,256]{2,1,0:T(8,128)(2,1)}) custom-call(s32[64]{0:T(128)S(1)} %copy-done.5, bf16[4,64,576]{2,1,0:T(8,128)(2,1)S(1)} %copy-done.3, bf16[4,576,256]{2,1,0:T(8,128)(2,1)S(1)} %bitcast.4), custom_call_target="tpu_custom_call" | custom-call | tf_op jit(solution)/shard_map/attend/pallas_call | solution.py:142
  85.9 1.3 %turn.1 = bf16[16,72,128]{2,1,0:T(8,128)(2,1)} custom-call(s32[3]{0:T(128)S(1)} %copy-done.4, bf16[16,72,128]{2,1,0:T(8,128)(2,1)S(1)} %all-to-all-done.pieces_ref), custom_call_target="tpu_custom_call" | custom-call | tf_op jit(solution)/shard_map/turn/pallas_call | solution.py:264
  87.3 4.1 %all-to-all-start.1 = ((bf16[16,72,128]{2,1,0:T(8,128)(2,1)}), bf16[16,72,128]{2,1,0:T(8,128)(2,1)S(1)}, u32[]{:S(2)}, u32[]{:S(2)}) async-start(bf16[16,72,128]{2,1,0:T(8,128)(2,1)} %turn.1), calls=%async_computation.1 | async-start | bytes 589824 | tf_op jit(solution)/shard_map/all_to_all | solution.py:320
  92.0 11.6 %all-to-all-done.1.pieces_ref = bf16[16,72,128]{2,1,0:T(8,128)(2,1)S(1)} async-done(((bf16[16,72,128]{2,1,0:T(8,128)(2,1)}), bf16[16,72,128]{2,1,0:T(8,128)(2,1)S(1)}, u32[]{:S(2)}, u32[]{:S(2)}) %all-to-all-start.1) | async-done | bytes 294944 | tf_op jit(solution)/shard_map/all_to_all | solution.py:320
  103.6 1.4 %patch_pieces.1 = bf16[4,576,256]{2,1,0:T(8,128)(2,1)} custom-call(s32[3]{0:T(128)S(1)} %copy-done.4, bf16[16,72,128]{2,1,0:T(8,128)(2,1)S(1)} %all-to-all-done.1.pieces_ref, bf16[4,576,256]{2,1,0:T(8,128)(2,1)} %patch_half.1.kept_ref), custom_call_target="tpu_custom_call", output_to_operand_aliasing={{}: (2, {})} | custom-call | tf_op jit(solution)/shard_map/patch_pieces/pallas_call | solution.py:307
  (40 shorter events, 8.5 us)
Async XLA Ops:
  3.5 4.4 %collective-permute-start.1 = (bf16[8,3840]{1,0:T(8,128)(2,1)}, bf16[8,3840]{1,0:T(8,128)(2,1)S(1)}, u32[]{:S(2)}, u32[]{:S(2)}) collective-permute-start(bf16[8,3840]{1,0:T(8,128)(2,1)} %get-tuple-element.21), channel_id=1, source_target_pairs={{0,1},{1,0},{2,3},{3,2},{4,5},{5,4},{6,7},{7,6},{8,9},{9,8},{10,11... | collective-permute-start | bytes 184328 | tf_op jit(solution)/shard_map/ppermute | solution.py:325
  8.7 5.2 %collective-permute-start.2 = (bf16[8,3840]{1,0:T(8,128)(2,1)S(1)}, bf16[8,3840]{1,0:T(8,128)(2,1)S(1)}, u32[]{:S(2)}, u32[]{:S(2)}) collective-permute-start(bf16[8,3840]{1,0:T(8,128)(2,1)S(1)} %add.35.own_ref), channel_id=1, source_target_pairs={{0,2},{1,15},{2,4},{3,1},{4,6},{5,3},{6,8},{7,5},{8,10},{9,7},{10,... | collective-permute-start | bytes 184328 | tf_op jit(solution)/shard_map/ppermute | solution.py:331
  14.0 5.6 %collective-permute-start.3 = (bf16[16,3840]{1,0:T(8,128)(2,1)S(1)}, bf16[16,3840]{1,0:T(8,128)(2,1)S(1)}, u32[]{:S(2)}, u32[]{:S(2)}) collective-permute-start(bf16[16,3840]{1,0:T(8,128)(2,1)S(1)} %pad_maximum_fusion), channel_id=1, source_target_pairs={{0,4},{1,13},{2,6},{3,15},{4,8},{5,1},{6,10},{7,3},{8,12},{9,5},{1... | collective-permute-start | bytes 368648 | tf_op jit(solution)/shard_map/ppermute | solution.py:331
  19.6 12.8 %collective-permute-start.6 = (bf16[16,3840]{1,0:T(8,128)(2,1)S(1)}, bf16[16,3840]{1,0:T(8,128)(2,1)S(1)}, u32[]{:S(2)}, u32[]{:S(2)}) collective-permute-start(bf16[16,3840]{1,0:T(8,128)(2,1)S(1)} %collective-permute-done.3.next_ref), channel_id=1, source_target_pairs={{0,1},{1,0},{2,3},{3,2},{4,5},{5,4},{6,7},{7,6},{8,9},{9,8},{10,11... | collective-permute-start | bytes 368648 | tf_op jit(solution)/shard_map/ppermute | solution.py:325
  23.2 6.7 %collective-permute-start.4 = (bf16[8,1920]{1,0:T(8,128)(2,1)S(1)}, bf16[8,1920]{1,0:T(8,128)(2,1)S(1)}, u32[]{:S(2)}, u32[]{:S(2)}) collective-permute-start(bf16[8,1920]{1,0:T(8,128)(2,1)S(1)} %slice_select_fusion.1), channel_id=1, source_target_pairs={{0,8},{1,9},{2,10},{3,11},{4,12},{5,13},{6,14},{7,15},{8,0},{9,1},... | collective-permute-start | bytes 92168 | tf_op jit(solution)/shard_map/ppermute | solution.py:331
  26.9 5.5 %collective-permute-start.5 = (bf16[8,3840]{1,0:T(8,128)(2,1)S(1)}, bf16[8,3840]{1,0:T(8,128)(2,1)S(1)}, u32[]{:S(2)}, u32[]{:S(2)}) collective-permute-start(bf16[8,3840]{1,0:T(8,128)(2,1)S(1)} %collective-permute-done.2.near_ref), channel_id=1, source_target_pairs={{0,1},{1,0},{2,3},{3,2},{4,5},{5,4},{6,7},{7,6},{8,9},{9,8},{10,11... | collective-permute-start | bytes 184328 | tf_op jit(solution)/shard_map/ppermute | solution.py:325
  29.8 2.5 %collective-permute-start.7 = (bf16[8,1920]{1,0:T(8,128)(2,1)S(1)}, bf16[8,1920]{1,0:T(8,128)(2,1)S(1)}, u32[]{:S(2)}, u32[]{:S(2)}) collective-permute-start(bf16[8,1920]{1,0:T(8,128)(2,1)S(1)} %collective-permute-done.4.far_ref), channel_id=1, source_target_pairs={{0,1},{1,0},{2,3},{3,2},{4,5},{5,4},{6,7},{7,6},{8,9},{9,8},{10,11... | collective-permute-start | bytes 92168 | tf_op jit(solution)/shard_map/ppermute | solution.py:325
  32.4 2.3 %copy-start.1 = (bf16[3584,640]{1,0:T(8,128)(2,1)S(1)}, bf16[3584,640]{1,0:T(8,128)(2,1)}, u32[]{:S(2)}) copy-start(bf16[3584,640]{1,0:T(8,128)(2,1)} %up_ref.1) | copy-start | bytes 13762564
  34.7 2.3 %copy-start.2 = (bf16[640,3584]{1,0:T(8,128)(2,1)S(1)}, bf16[640,3584]{1,0:T(8,128)(2,1)}, u32[]{:S(2)}) copy-start(bf16[640,3584]{1,0:T(8,128)(2,1)} %down_ref.1) | copy-start | bytes 13762564
  37.0 11.3 %copy-start.7 = (bf16[576,256]{1,0:T(8,128)(2,1)S(1)}, bf16[576,256]{1,0:T(8,128)(2,1)}, u32[]{:S(2)}) copy-start(bf16[576,256]{1,0:T(8,128)(2,1)} %get-tuple-element.19) | copy-start | bytes 884740
  42.6 11.6 %collective-permute-start.8 = (f32[24,3584]{1,0:T(8,128)S(1)}, f32[24,3584]{1,0:T(8,128)S(1)}, u32[]{:S(2)}, u32[]{:S(2)}) collective-permute-start(f32[24,3584]{1,0:T(8,128)S(1)} %get-tuple-element.24), channel_id=1, source_target_pairs={{0,1},{1,0},{2,3},{3,2},{4,5},{5,4},{6,7},{7,6},{8,9},{9,8},{10,11... | collective-permute-start | bytes 1032200 | tf_op jit(solution)/shard_map/ppermute | solution.py:325
  43.1 38.2 %copy-start = (bf16[4,256,576]{1,2,0:T(8,128)(2,1)S(1)}, bf16[4,256,576]{1,2,0:T(8,128)(2,1)}, u32[]{:S(2)}) copy-start(bf16[4,256,576]{1,2,0:T(8,128)(2,1)} %param.11) | copy-start | bytes 3538948
  43.1 38.2 %copy-start.3 = (bf16[4,64,576]{2,1,0:T(8,128)(2,1)S(1)}, bf16[4,64,576]{2,1,0:T(8,128)(2,1)}, u32[]{:S(2)}) copy-start(bf16[4,64,576]{2,1,0:T(8,128)(2,1)} %queries_ref.1) | copy-start | bytes 884740
  43.1 38.2 %copy-start.5 = (s32[64]{0:T(128)S(1)}, s32[64]{0:T(128)}, u32[]{:S(2)}) copy-start(s32[64]{0:T(128)} %lengths_ref.1) | copy-start | bytes 772
  43.1 42.8 %all-to-all-start = ((bf16[16,72,128]{2,1,0:T(8,128)(2,1)}), bf16[16,72,128]{2,1,0:T(8,128)(2,1)S(1)}, u32[]{:S(2)}, u32[]{:S(2)}) async-start(bf16[16,72,128]{2,1,0:T(8,128)(2,1)} %get-tuple-element.18), calls=%async_computation | async-start | bytes 589824 | tf_op jit(solution)/shard_map/all_to_all | solution.py:320
  48.3 36.4 %collective-permute-start = (bf16[576,256]{1,0:T(8,128)(2,1)S(1)}, bf16[576,256]{1,0:T(8,128)(2,1)S(1)}, u32[]{:S(2)}, u32[]{:S(2)}) collective-permute-start(bf16[576,256]{1,0:T(8,128)(2,1)S(1)} %copy-done.7), channel_id=1, source_target_pairs={{0,8},{1,9},{2,10},{3,11},{4,12},{5,13},{6,14},{7,15},{8,0},{9,1},... | collective-permute-start | bytes 884744 | tf_op jit(solution)/shard_map/ppermute | solution.py:31
  53.6 1.6 %collective-permute-start.11 = (f32[8,1792]{1,0:T(8,128)S(1)}, f32[8,1792]{1,0:T(8,128)S(1)}, u32[]{:S(2)}, u32[]{:S(2)}) collective-permute-start(f32[8,1792]{1,0:T(8,128)S(1)} %get-tuple-element.26), channel_id=1, source_target_pairs={{0,1},{1,0},{2,3},{3,2},{4,5},{5,4},{6,7},{7,6},{8,9},{9,8},{10,11... | collective-permute-start | bytes 172040 | tf_op jit(solution)/shard_map/ppermute | solution.py:325
  54.3 8.2 %collective-permute-start.9 = (f16[16,3584]{1,0:T(8,128)(2,1)S(1)}, f16[16,3584]{1,0:T(8,128)(2,1)S(1)}, u32[]{:S(2)}, u32[]{:S(2)}) collective-permute-start(f16[16,3584]{1,0:T(8,128)(2,1)S(1)} %fusion.1), channel_id=1, source_target_pairs={{0,4},{1,13},{2,6},{3,15},{4,8},{5,1},{6,10},{7,3},{8,12},{9,5},{1... | collective-permute-start | bytes 344072 | tf_op jit(solution)/shard_map/ppermute | solution.py:331
  55.2 20.4 %collective-permute-start.12 = (f16[8,1792]{1,0:T(8,128)(2,1)S(1)}, f16[8,1792]{1,0:T(8,128)(2,1)S(1)}, u32[]{:S(2)}, u32[]{:S(2)}) collective-permute-start(f16[8,1792]{1,0:T(8,128)(2,1)S(1)} %multiply_convert_fusion), channel_id=1, source_target_pairs={{0,8},{1,9},{2,10},{3,11},{4,12},{5,13},{6,14},{7,15},{8,0},{9,1},... | collective-permute-start | bytes 86024 | tf_op jit(solution)/shard_map/ppermute | solution.py:331
  62.6 22.1 %copy-start.4 = (s32[3]{0:T(128)S(1)}, s32[3]{0:T(128)}, u32[]{:S(2)}) copy-start(s32[3]{0:T(128)} %get-tuple-element.17.info_ref) | copy-start | bytes 40
  62.6 14.3 %collective-permute-start.10 = (f16[8,3584]{1,0:T(8,128)(2,1)S(1)}, f16[8,3584]{1,0:T(8,128)(2,1)S(1)}, u32[]{:S(2)}, u32[]{:S(2)}) collective-permute-start(f16[8,3584]{1,0:T(8,128)(2,1)S(1)} %fusion.4), channel_id=1, source_target_pairs={{0,2},{1,15},{2,4},{3,1},{4,6},{5,3},{6,8},{7,5},{8,10},{9,7},{10,... | collective-permute-start | bytes 172040 | tf_op jit(solution)/shard_map/ppermute | solution.py:331
  76.9 14.4 %collective-permute-start.13 = (f32[4,3584]{1,0:T(4,128)S(1)}, f32[4,3584]{1,0:T(4,128)S(1)}, u32[]{:S(2)}, u32[]{:S(2)}) collective-permute-start(f32[4,3584]{1,0:T(4,128)S(1)} %slice_select_fusion), channel_id=1, source_target_pairs={{0,1},{1,0},{2,3},{3,2},{4,5},{5,4},{6,7},{7,6},{8,9},{9,8},{10,11... | collective-permute-start | bytes 172040 | tf_op jit(solution)/shard_map/ppermute | solution.py:325
  85.9 5.4 %copy-start.6 = (bf16[4,3584]{1,0:T(4,128)(2,1)S(1)}, bf16[4,3584]{1,0:T(4,128)(2,1)}, u32[]{:S(2)}) copy-start(bf16[4,3584]{1,0:T(4,128)(2,1)} %hidden_ref.1) | copy-start | bytes 86020
  87.3 16.4 %all-to-all-start.1 = ((bf16[16,72,128]{2,1,0:T(8,128)(2,1)}), bf16[16,72,128]{2,1,0:T(8,128)(2,1)S(1)}, u32[]{:S(2)}, u32[]{:S(2)}) async-start(bf16[16,72,128]{2,1,0:T(8,128)(2,1)} %turn.1), calls=%async_computation.1 | async-start | bytes 589824 | tf_op jit(solution)/shard_map/all_to_all | solution.py:320

commit v2 on v1

--- a/solution.py
+++ b/solution.py
@@ -21,6 +21,14 @@
 HBM = pltpu.HBM
 
 
+def in_hbm(x):
+    return pltpu.with_memory_space_constraint(x, HBM)
+
+
+def in_vmem(x):
+    return pltpu.with_memory_space_constraint(x, VMEM)
+
+
 def whole(space):
     return pl.BlockSpec(memory_space=space)
 
@@ -40,33 +48,9 @@
     ]
 
 
-def prepare_kernel(
-    devices, moves_ref, cache_ref, hidden_ref, gain_ref, queue_ref, deadline_ref,
-    half_ref, pieces_ref, rows_ref, info_ref, sems,
-):
+def rows_kernel(hidden_ref, gain_ref, queue_ref, deadline_ref, rows_ref):
     me = lax.axis_index("dev")
-    own_rows = cache_ref.shape[0]
-    leaving = [moves_ref[0, j * devices + me] - me * own_rows for j in range(2)]
-    distance = [
-        (moves_ref[2, j * devices + me] - me + devices) % devices for j in range(2)
-    ]
-    first_is_half = distance[0] == devices // 2
-    half_row = jnp.where(first_is_half, leaving[0], leaving[1])
-    other_row = jnp.where(first_is_half, leaving[1], leaving[0])
-    info_ref[0] = jnp.where(first_is_half, distance[1], distance[0])
-    info_ref[1] = half_row
-    info_ref[2] = other_row
-    copies = [
-        pltpu.make_async_copy(cache_ref.at[half_row], half_ref, sems.at[0]),
-    ] + [
-        pltpu.make_async_copy(
-            cache_ref.at[other_row, rows, lanes], pieces_ref.at[i], sems.at[1 + i]
-        )
-        for i, (rows, lanes) in enumerate(piece_windows(*pieces_ref.shape))
-    ]
-    for copy in copies:
-        copy.start()
-    features = hidden_ref.shape[1]
+    own_rows, features = hidden_ref.shape
     wide = hidden_ref[...].astype(jnp.float32)
     scaled = lax.rsqrt(jnp.mean(wide * wide, axis=-1, keepdims=True) + 1e-06)
     normed = wide * scaled * gain_ref[...].astype(jnp.float32)[None, :]
@@ -85,42 +69,64 @@
         counts = jnp.where(lane == b, count, counts)
     counts = jnp.where(row == (me % 2) * own_rows, counts, 0)
     rows_ref[:, features:] = counts.astype(jnp.float32).astype(jnp.bfloat16)
+
+
+def make_rows(hidden_in, norm_gain, queue_counts, deadline):
+    own_rows, features = hidden_in.shape
+    return pl.pallas_call(
+        rows_kernel,
+        out_shape=pltpu.VMEM((2 * own_rows, features + 2 * LANES), jnp.bfloat16),
+        in_specs=[whole(VMEM), whole(VMEM), whole(SMEM), whole(SMEM)],
+        out_specs=whole(VMEM),
+        name="rows",
+    )(hidden_in, norm_gain, queue_counts, deadline)
+
+
+def payload_kernel(devices, moves_ref, cache_ref, half_ref, pieces_ref, info_ref, sems):
+    me = lax.axis_index("dev")
+    own_rows = cache_ref.shape[0]
+    leaving = [moves_ref[0, j * devices + me] - me * own_rows for j in range(2)]
+    distance = [
+        (moves_ref[2, j * devices + me] - me + devices) % devices for j in range(2)
+    ]
+    first_is_half = distance[0] == devices // 2
+    half_row = jnp.where(first_is_half, leaving[0], leaving[1])
+    other_row = jnp.where(first_is_half, leaving[1], leaving[0])
+    info_ref[0] = jnp.where(first_is_half, distance[1], distance[0])
+    info_ref[1] = half_row
+    info_ref[2] = other_row
+    copies = [
+        pltpu.make_async_copy(
+            cache_ref.at[other_row, rows, lanes], pieces_ref.at[i], sems.at[1 + i]
+        )
+        for i, (rows, lanes) in enumerate(piece_windows(*pieces_ref.shape))
+    ]
+    copies.append(pltpu.make_async_copy(cache_ref.at[half_row], half_ref, sems.at[0]))
+    for copy in copies:
+        copy.start()
     for copy in copies:
         copy.wait()
 
 
-def prepare(moves, cache, hidden_in, norm_gain, queue_counts, deadline):
+def make_payload(moves, cache):
     devices = lax.axis_size("dev")
-    own_rows, depth, context = cache.shape
-    features = hidden_in.shape[1]
-    return pl.pallas_call(
-        partial(prepare_kernel, devices),
+    _, depth, context = cache.shape
+    return pl.pallas_call(
+        partial(payload_kernel, devices),
         out_shape=(
-            jax.ShapeDtypeStruct((depth, context), cache.dtype),
-            jax.ShapeDtypeStruct(
-                (devices, depth * context // (devices * LANES), LANES), cache.dtype
-            ),
-            jax.ShapeDtypeStruct((2 * own_rows, features + 2 * LANES), jnp.bfloat16),
+            pltpu.VMEM((depth, context), cache.dtype),
+            pltpu.VMEM((devices, depth * context // (devices * LANES), LANES), cache.dtype),
             jax.ShapeDtypeStruct((3,), jnp.int32),
         ),
-        in_specs=[
-            whole(SMEM), whole(HBM), whole(VMEM), whole(VMEM), whole(SMEM), whole(SMEM),
-        ],
-        out_specs=(whole(VMEM), whole(VMEM), whole(VMEM), whole(SMEM)),
+        in_specs=[whole(SMEM), whole(HBM)],
+        out_specs=(whole(VMEM), whole(VMEM), whole(SMEM)),
         scratch_shapes=[pltpu.SemaphoreType.DMA((devices + 1,))],
-        name="prepare",
-    )(moves, cache, hidden_in, norm_gain, queue_counts, deadline)
-
-
-def attend_kernel(lengths_ref, queries_ref, cache_ref, out_ref, kept_ref):
-    own_rows = pl.num_programs(0)
-    row = pl.program_id(0)
-    length = lengths_ref[lax.axis_index("dev") * own_rows + row]
-    latent = cache_ref[0]
-    kept_ref[0] = latent
-    scores = (
-        jnp.dot(queries_ref[0], latent, preferred_element_type=jnp.float32) * softmax_scale
-    )
+        name="payload",
+    )(moves, in_hbm(cache))
+
+
+def attention(queries, latent, length):
+    scores = jnp.dot(queries, latent, preferred_element_type=jnp.float32) * softmax_scale
     included = lax.broadcasted_iota(jnp.int32, scores.shape, 1) < length
     scores = jnp.where(included, scores, jnp.float32(-1e30))
     largest = jnp.max(scores, axis=-1, keepdims=True)
@@ -132,49 +138,87 @@
         (((1,), (1,)), ((), ())),
         preferred_element_type=jnp.float32,
     )
-    out_ref[0] = (summed / total).astype(jnp.bfloat16)
-
-
-def attend(lengths, queries, cache):
-    own_rows, heads, depth = queries.shape
-    context = cache.shape[2]
-    block = lambda *dims: pl.BlockSpec((1, *dims), lambda r: (r, 0, 0))
+    return (summed / total).astype(jnp.bfloat16)
+
+
+def attend_kernel(
+    lengths_ref, queries_ref, cache_ref, up_ref, down_ref,
+    attn_ref, kept_ref, up_out, down_out,
+    queries_buf, cache_buf, attn_buf, lengths_buf,
+    in_sems, kept_sems, attn_sems, weight_sems, lengths_sem,
+):
+    own_rows = queries_buf.shape[0]
+    me = lax.axis_index("dev")
+    lengths_copy = pltpu.make_async_copy(lengths_ref, lengths_buf, lengths_sem)
+    lengths_copy.start()
+    in_copies = [
+        (
+            pltpu.make_async_copy(cache_ref.at[r], cache_buf.at[r], in_sems.at[2 * r]),
+            pltpu.make_async_copy(queries_ref.at[r], queries_buf.at[r], in_sems.at[2 * r + 1]),
+        )
+        for r in range(own_rows)
+    ]
+    out_copies = [
+        pltpu.make_async_copy(up_ref, up_out, weight_sems.at[0]),
+        pltpu.make_async_copy(down_ref, down_out, weight_sems.at[1]),
+    ]
+    for pair in in_copies:
+        for copy in pair:
+            copy.start()
+    for copy in out_copies:
+        copy.start()
+    lengths_copy.wait()
+    for r in range(own_rows):
+        for copy in in_copies[r]:
+            copy.wait()
+        kept = pltpu.make_async_copy(cache_buf.at[r], kept_ref.at[r], kept_sems.at[r])
+        kept.start()
+        attn_buf[r] = attention(
+            queries_buf[r], cache_buf[r], lengths_buf[me * own_rows + r]
+        )
+        done = pltpu.make_async_copy(attn_buf.at[r], attn_ref.at[r], attn_sems.at[r])
+        done.start()
+        out_copies += [kept, done]
+    for copy in out_copies:
+        copy.wait()
+
+
+def attend(lengths, queries, cache, w_up, w_down):
+    own_rows, heads, _ = queries.shape
     return pl.pallas_call(
         attend_kernel,
-        grid=(own_rows,),
         out_shape=(
             jax.ShapeDtypeStruct((own_rows, heads, VL), jnp.bfloat16),
             jax.ShapeDtypeStruct(cache.shape, cache.dtype),
+            pltpu.VMEM(w_up.shape, w_up.dtype),
+            pltpu.VMEM(w_down.shape, w_down.dtype),
         ),
-        in_specs=[whole(SMEM), block(heads, depth), block(depth, context)],
-        out_specs=(block(heads, VL), block(depth, context)),
+        in_specs=[whole(HBM)] * 5,
+        out_specs=(whole(HBM),) * 2 + (whole(VMEM),) * 2,
+        scratch_shapes=[
+            pltpu.VMEM(queries.shape, queries.dtype),
+            pltpu.VMEM(cache.shape, cache.dtype),
+            pltpu.VMEM((own_rows, heads, VL), jnp.bfloat16),
+            pltpu.SMEM(lengths.shape, jnp.int32),
+            pltpu.SemaphoreType.DMA((2 * own_rows,)),
+            pltpu.SemaphoreType.DMA((own_rows,)),
+            pltpu.SemaphoreType.DMA((own_rows,)),
+            pltpu.SemaphoreType.DMA((2,)),
+            pltpu.SemaphoreType.DMA,
+        ],
         compiler_params=pltpu.CompilerParams(vmem_limit_bytes=12 * MIB),
         name="attend",
-    )(lengths, queries, cache)
+    )(in_hbm(lengths), in_hbm(queries), in_hbm(cache), in_hbm(w_up), in_hbm(w_down))
 
 
 def feed_kernel(
+    up_ref, down_ref,
     own_ref, near_ref, next_ref, far_ref, other_near_ref, other_next_ref, other_far_ref,
-    up_ref, down_ref,
     own_out, give_out, keep_out, give_far_out, keep_far_out, load_ref,
-    rows_buf, up_buf, down_buf, up_sems, down_sems,
+    rows_buf,
 ):
-    pieces, depth, _ = up_buf.shape
-    columns = down_buf.shape[2]
-    up_copies = [
-        pltpu.make_async_copy(
-            up_ref.at[pl.ds(i * depth, depth), :], up_buf.at[i], up_sems.at[i]
-        )
-        for i in range(pieces)
-    ]
-    down_copies = [
-        pltpu.make_async_copy(
-            down_ref.at[:, pl.ds(i * columns, columns)], down_buf.at[i], down_sems.at[i]
-        )
-        for i in range(down_buf.shape[0])
-    ]
-    for copy in up_copies + down_copies:
-        copy.start()
+    features, _ = up_ref.shape
+    columns = features // 7
     first_core = lax.axis_index("dev") % 2 == 0
     block = own_ref.shape[0]
     width = own_ref.shape[1]
@@ -186,24 +230,14 @@
     other_far = other_far_ref[...]
     rows_buf[7 * block :, 0 : width // 2] = jnp.where(first_core, far, other_far)
     rows_buf[7 * block :, width // 2 :] = jnp.where(first_core, other_far, far)
-    features = pieces * depth
     counts = rows_buf[:, features : features + LANES].astype(jnp.float32)
     load_ref[...] = jnp.sum(counts, axis=0)[0:BUCKETS]
-    up = None
-    for i in range(pieces):
-        up_copies[i].wait()
-        term = jnp.dot(
-            rows_buf[:, i * depth : (i + 1) * depth],
-            up_buf[i],
-            preferred_element_type=jnp.float32,
-        )
-        up = term if up is None else up + term
+    up = jnp.dot(rows_buf[:, 0:features], up_ref[...], preferred_element_type=jnp.float32)
     hidden = (up / (1.0 + jnp.exp(-up))).astype(jnp.bfloat16)
     half = features // 2
-    for i, copy in enumerate(down_copies):
-        copy.wait()
-        product = jnp.dot(hidden, down_buf[i], preferred_element_type=jnp.float32)
+    for i in range(features // columns):
         at = slice(i * columns, (i + 1) * columns)
+        product = jnp.dot(hidden, down_ref[:, at], preferred_element_type=jnp.float32)
         own_out[:, at] = product[0:block]
         give_out[:, at] = product[block : 4 * block]
         keep_out[:, at] = product[4 * block : 7 * block]
@@ -224,12 +258,10 @@
                     give_far_out[:, target] = piece
 
 
-def feed(parts, w_up, w_down):
-    features, units = w_up.shape
-    pieces = 7
-    depth = features // pieces
-    block, width = parts[0].shape
-    wide = lambda rows, columns: jax.ShapeDtypeStruct((rows, columns), jnp.float32)
+def feed(w_up, w_down, parts):
+    features, _ = w_up.shape
+    block, row_width = parts[0].shape
+    wide = lambda rows, columns: pltpu.VMEM((rows, columns), jnp.float32)
     return pl.pallas_call(
         feed_kernel,
         out_shape=(
@@ -240,24 +272,26 @@
             wide(block, features // 2),
             jax.ShapeDtypeStruct((BUCKETS,), jnp.float32),
         ),
-        in_specs=[whole(VMEM)] * 7 + [whole(HBM)] * 2,
+        in_specs=[whole(VMEM)] * 9,
         out_specs=(whole(VMEM),) * 6,
-        scratch_shapes=[
-            pltpu.VMEM((8 * block, width), jnp.bfloat16),
-            pltpu.VMEM((pieces, depth, units), w_up.dtype),
-            pltpu.VMEM((pieces, units, depth), w_down.dtype),
-            pltpu.SemaphoreType.DMA((pieces,)),
-            pltpu.SemaphoreType.DMA((pieces,)),
-        ],
-        compiler_params=pltpu.CompilerParams(vmem_limit_bytes=20 * MIB),
+        scratch_shapes=[pltpu.VMEM((8 * block, row_width), jnp.bfloat16)],
+        compiler_params=pltpu.CompilerParams(vmem_limit_bytes=12 * MIB),
         name="feed",
-    )(*parts, w_up, w_down)
-
-
-def turn_kernel(devices, info_ref, pieces_ref, out_ref):
+    )(in_vmem(w_up), in_vmem(w_down), *parts)
+
+
+def turn_kernel(devices, info_ref, pieces_ref, out_ref, sems):
     steps = info_ref[0]
-    for d in range(devices):
-        out_ref[d] = pieces_ref[(d - steps + devices) % devices]
+    copies = [
+        pltpu.make_async_copy(
+            pieces_ref.at[(d - steps + devices) % devices], out_ref.at[d], sems.at[d]
+        )
+        for d in range(devices)
+    ]
+    for copy in copies:
+        copy.start()
+    for copy in copies:
+        copy.wait()
 
 
 def turn(info, pieces):
@@ -265,10 +299,11 @@
         partial(turn_kernel, pieces.shape[0]),
         out_shape=jax.ShapeDtypeStruct(pieces.shape, pieces.dtype),
         in_specs=[whole(SMEM), whole(VMEM)],
-        out_specs=whole(VMEM),
+        out_specs=whole(HBM),
+        scratch_shapes=[pltpu.SemaphoreType.DMA((pieces.shape[0],))],
         compiler_params=pltpu.CompilerParams(vmem_limit_bytes=4 * MIB),
         name="turn",
-    )(info, pieces)
+    )(info, in_vmem(pieces))
 
 
 def patch_half_kernel(info_ref, half_ref, kept_ref, out_ref, sem):
@@ -350,22 +385,21 @@
     first_core = lax.axis_index("dev") % 2 == 0
     block = 2 * own_rows
     cache = jnp.swapaxes(latent_cache, 1, 2)
-    half, pieces, rows, info = prepare(
-        moves.T, cache, hidden_in, norm_gain, queue_counts, deadline
-    )
+    rows = make_rows(hidden_in, norm_gain, queue_counts, deadline)
     own = rows + swapped(rows)
+    half, pieces, info = make_payload(moves.T, cache)
     width = own.shape[1] // 2
     far = outward(jnp.where(first_core, own[:, :width], own[:, width:]), 4)
     near = outward(own, 1)
     pieces = exchange(pieces)
     nxt = outward(jnp.concatenate([own, near], axis=0), 2)
     half = shifted(half, "dev", devices // 2)
-    attn_out, kept = attend(lengths, q_lat, cache)
     other_near = swapped(near)
     other_far = swapped(far)
     other_next = swapped(nxt)
+    attn_out, kept, w_up, w_down = attend(lengths, q_lat, cache, w_up, w_down)
     own_sums, give, keep, give_far, keep_far, load = feed(
-        (own, near, nxt, far, other_near, other_next, other_far), w_up, w_down
+        w_up, w_down, (own, near, nxt, far, other_near, other_next, other_far)
     )
     pieces = turn(info, pieces)
     got_far = swapped(give_far)

time: 105 us -> 94.2 us (0.90)
  starting transfers between devices: 55.2 us -> 40.4 us
  waiting for transfers between devices: 26.9 us -> 35.4 us
  local copies, waits for them, and re-layouts: 4.63 us -> 0.67 us
    ppermute x6, waiting for transfers between devices: 12.8 us -> 22.9 us  [outward(): return lax.ppermute(value, 'dev', pairs)]
    ppermute x6, starting transfers between devices: 26.3 us -> 16.6 us  [outward(): return lax.ppermute(value, 'dev', pairs)]
    unnamed x16 -> x6, local copies, waits for them, and re-layouts: 4.63 us -> 0.67 us
    pallas_call x1, Pallas kernels: 5.68 us -> 3 us  [feed(): pl.pallas_call(feed_kernel, out_shape=(wide(block, features), wide(3 * bl...]
    ppermute x7, starting transfers between devices: 14.3 us -> 11.7 us  [swapped(): return lax.ppermute(value, 'dev', [(s, s ^ 1) for s in range(count)])]
    pallas_call x2 -> x3, Pallas kernels: 6.21 us -> 8.63 us  [the longest x1 4.83 us: attend(): pl.pallas_call(attend_kernel, out_shape=(jax.ShapeDtypeStruct((own_rows,...]
    ppermute x1, starting transfers between devices: 5.35 us -> 3.39 us  [shifted(): return lax.ppermute(value, axis, pairs)]
    ppermute x7, waiting for transfers between devices: 2.47 us -> 0.91 us  [swapped(): return lax.ppermute(value, 'dev', [(s, s ^ 1) for s in range(count)])]
  transfers between devices with their start and end apart: 16 -> 16, of which waited for: 9 -> 7; matrix products, arithmetic and copies ran while one was open for 1% -> 1% of each run, Pallas kernels for 6% -> 11%
where the time goes in v2:
time: 94.2 us; the launch traced here: 93.8 us
  starting transfers between devices  40.4 us (43%)
  waiting for transfers between devices  35.4 us (38%)
  Pallas kernels  15.7 us (17%)
    ppermute x6, waiting for transfers between devices, outward(): return lax.ppermute(value, 'dev', pairs)  22.9 us
    ppermute x6, starting transfers between devices, outward(): return lax.ppermute(value, 'dev', pairs)  16.6 us
    ppermute x7, starting transfers between devices, swapped(): return lax.ppermute(value, 'dev', [(s, s ^ 1) for s in range(count)])  11.7 us
    all_to_all x2, waiting for transfers between devices, exchange(): return lax.all_to_all(value, 'dev', 0, 0, tiled=True)  11.6 us
    all_to_all x2, starting transfers between devices, exchange(): return lax.all_to_all(value, 'dev', 0, 0, tiled=True)  8.72 us
    pallas_call x1, Pallas kernels, attend(): pl.pallas_call(attend_kernel, out_shape=(jax.ShapeDtypeStruct((own_rows,...  4.83 us
    ppermute x1, starting transfers between devices, shifted(): return lax.ppermute(value, axis, pairs)  3.39 us
    pallas_call x1, Pallas kernels, feed(): pl.pallas_call(feed_kernel, out_shape=(wide(block, features), wide(3 * bl...  3 us
  transfers between devices with their start and end apart: 16, of which 7 were waited for; matrix products, arithmetic and copies ran while one was open for 1% of the time, Pallas kernels for 11%

profile of v2, /device:TPU:1, one launch (start us, length us, event | category | flops | bytes accessed | tf_op | source)
XLA Modules:
  0.0 93.8 jit_solution(5023361158765845794)
XLA Ops:
  1.6 3.3 %collective-permute-start.1 = (bf16[8,3840]{1,0:T(8,128)(2,1)S(1)}, bf16[8,3840]{1,0:T(8,128)(2,1)S(1)}, u32[]{:S(2)}, u32[]{:S(2)}) collective-permute-start(bf16[8,3840]{1,0:T(8,128)(2,1)S(1)} %rows.1), channel_id=1, source_target_pairs={{0,1},{1,0},{2,3},{3,2},{4,5},{5,4},{6,7},{7,6},{8,9},{9,8},{10,11... | collective-permute-start | bytes 184328 | tf_op jit(solution)/shard_map/ppermute | solution.py:360
  5.8 3.9 %collective-permute-start.2 = (bf16[8,3840]{1,0:T(8,128)(2,1)S(1)}, bf16[8,3840]{1,0:T(8,128)(2,1)S(1)}, u32[]{:S(2)}, u32[]{:S(2)}) collective-permute-start(bf16[8,3840]{1,0:T(8,128)(2,1)S(1)} %add.35.own_ref), channel_id=1, source_target_pairs={{0,2},{1,15},{2,4},{3,1},{4,6},{5,3},{6,8},{7,5},{8,10},{9,7},{10,... | collective-permute-start | bytes 184328 | tf_op jit(solution)/shard_map/ppermute | solution.py:366
  9.7 1.3 %collective-permute-done.2.near_ref = bf16[8,3840]{1,0:T(8,128)(2,1)S(1)} collective-permute-done((bf16[8,3840]{1,0:T(8,128)(2,1)S(1)}, bf16[8,3840]{1,0:T(8,128)(2,1)S(1)}, u32[]{:S(2)}, u32[]{:S(2)}) %collective-permute-start.2) | collective-permute-done | bytes 61472 | tf_op jit(solution)/shard_map/ppermute | solution.py:366
  11.0 2.3 %collective-permute-start.3 = (bf16[16,3840]{1,0:T(8,128)(2,1)S(1)}, bf16[16,3840]{1,0:T(8,128)(2,1)S(1)}, u32[]{:S(2)}, u32[]{:S(2)}) collective-permute-start(bf16[16,3840]{1,0:T(8,128)(2,1)S(1)} %pad_maximum_fusion), channel_id=1, source_target_pairs={{0,4},{1,13},{2,6},{3,15},{4,8},{5,1},{6,10},{7,3},{8,12},{9,5},{1... | collective-permute-start | bytes 368648 | tf_op jit(solution)/shard_map/ppermute | solution.py:366
  13.3 3.3 %collective-permute-done.3.next_ref = bf16[16,3840]{1,0:T(8,128)(2,1)S(1)} collective-permute-done((bf16[16,3840]{1,0:T(8,128)(2,1)S(1)}, bf16[16,3840]{1,0:T(8,128)(2,1)S(1)}, u32[]{:S(2)}, u32[]{:S(2)}) %collective-permute-start.3) | collective-permute-done | bytes 122912 | tf_op jit(solution)/shard_map/ppermute | solution.py:366
  16.6 3.6 %collective-permute-start.6 = (bf16[16,3840]{1,0:T(8,128)(2,1)S(1)}, bf16[16,3840]{1,0:T(8,128)(2,1)S(1)}, u32[]{:S(2)}, u32[]{:S(2)}) collective-permute-start(bf16[16,3840]{1,0:T(8,128)(2,1)S(1)} %collective-permute-done.3.next_ref), channel_id=1, source_target_pairs={{0,1},{1,0},{2,3},{3,2},{4,5},{5,4},{6,7},{7,6},{8,9},{9,8},{10,11... | collective-permute-start | bytes 368648 | tf_op jit(solution)/shard_map/ppermute | solution.py:360
  20.2 3.7 %collective-permute-start.4 = (bf16[8,1920]{1,0:T(8,128)(2,1)S(1)}, bf16[8,1920]{1,0:T(8,128)(2,1)S(1)}, u32[]{:S(2)}, u32[]{:S(2)}) collective-permute-start(bf16[8,1920]{1,0:T(8,128)(2,1)S(1)} %slice_select_fusion.1), channel_id=1, source_target_pairs={{0,8},{1,9},{2,10},{3,11},{4,12},{5,13},{6,14},{7,15},{8,0},{9,1},... | collective-permute-start | bytes 92168 | tf_op jit(solution)/shard_map/ppermute | solution.py:366
  24.3 2.6 %collective-permute-done.4.far_ref = bf16[8,1920]{1,0:T(8,128)(2,1)S(1)} collective-permute-done((bf16[8,1920]{1,0:T(8,128)(2,1)S(1)}, bf16[8,1920]{1,0:T(8,128)(2,1)S(1)}, u32[]{:S(2)}, u32[]{:S(2)}) %collective-permute-start.4) | collective-permute-done | bytes 30752 | tf_op jit(solution)/shard_map/ppermute | solution.py:366
  26.9 1.7 %collective-permute-start.7 = (bf16[8,1920]{1,0:T(8,128)(2,1)S(1)}, bf16[8,1920]{1,0:T(8,128)(2,1)S(1)}, u32[]{:S(2)}, u32[]{:S(2)}) collective-permute-start(bf16[8,1920]{1,0:T(8,128)(2,1)S(1)} %collective-permute-done.4.far_ref), channel_id=1, source_target_pairs={{0,1},{1,0},{2,3},{3,2},{4,5},{5,4},{6,7},{7,6},{8,9},{9,8},{10,11... | collective-permute-start | bytes 92168 | tf_op jit(solution)/shard_map/ppermute | solution.py:360
  28.5 4.8 %attend.1 = (bf16[4,64,512]{2,1,0:T(8,128)(2,1)}, bf16[4,576,256]{2,1,0:T(8,128)(2,1)}, bf16[3584,640]{1,0:T(8,128)(2,1)S(1)}, bf16[640,3584]{1,0:T(8,128)(2,1)S(1)}) custom-call(s32[64]{0:T(128)} %lengths_ref.1, bf16[4,64,576]{2,1,0:T(8,128)(2,1)} %queries_ref.1, bf16[4,576,256]{2,1,0:T(8,128)(2,1)} %bitcast.4, bf16[3584,640]{1,0:T(8,128)(2,1)} %up_ref.1, ...), custom_call_target="tpu_custom_call" | custom-call | tf_op jit(solution)/shard_map/attend/pallas_call | solution.py:188
  33.4 3.0 %feed.1 = (f32[8,3584]{1,0:T(8,128)S(1)}, f32[24,3584]{1,0:T(8,128)S(1)}, f32[24,3584]{1,0:T(8,128)S(1)}, f32[8,1792]{1,0:T(8,128)S(1)}, f32[8,1792]{1,0:T(8,128)S(1)}, /*index=5*/f32[8]{0:T(128)}) custom-call(bf16[3584,640]{1,0:T(8,128)(2,1)S(1)} %get-tuple-element.22.up_ref, bf16[640,3584]{1,0:T(8,128)(2,1)S(1)} %get-tuple-element.23.down_ref, ...), custom_call_target="tpu_custom_call" | custom-call | tf_op jit(solution)/shard_map/feed/pallas_call | solution.py:265
  36.4 2.9 %payload.1 = (bf16[576,256]{1,0:T(8,128)(2,1)S(1)}, bf16[16,72,128]{2,1,0:T(8,128)(2,1)}, s32[3]{0:T(128)}) custom-call(s32[3,32]{1,0:T(4,128)} %bitcast.6, bf16[4,576,256]{2,1,0:T(8,128)(2,1)} %bitcast.5), custom_call_target="tpu_custom_call" | custom-call | tf_op jit(solution)/shard_map/payload/pallas_call | solution.py:114
  39.3 3.4 %collective-permute-start = (bf16[576,256]{1,0:T(8,128)(2,1)S(1)}, bf16[576,256]{1,0:T(8,128)(2,1)S(1)}, u32[]{:S(2)}, u32[]{:S(2)}) collective-permute-start(bf16[576,256]{1,0:T(8,128)(2,1)S(1)} %get-tuple-element.20), channel_id=1, source_target_pairs={{0,8},{1,9},{2,10},{3,11},{4,12},{5,13},{6,14},{7,15},{8,0},{9,1},... | collective-permute-start | bytes 884744 | tf_op jit(solution)/shard_map/ppermute | solution.py:39
  42.7 4.3 %all-to-all-start = ((bf16[16,72,128]{2,1,0:T(8,128)(2,1)}), bf16[16,72,128]{2,1,0:T(8,128)(2,1)S(1)}, u32[]{:S(2)}, u32[]{:S(2)}) async-start(bf16[16,72,128]{2,1,0:T(8,128)(2,1)} %get-tuple-element.19), calls=%async_computation | async-start | bytes 589824 | tf_op jit(solution)/shard_map/all_to_all | solution.py:355
  47.2 3.8 %collective-permute-start.9 = (f16[16,3584]{1,0:T(8,128)(2,1)S(1)}, f16[16,3584]{1,0:T(8,128)(2,1)S(1)}, u32[]{:S(2)}, u32[]{:S(2)}) collective-permute-start(f16[16,3584]{1,0:T(8,128)(2,1)S(1)} %fusion.1), channel_id=1, source_target_pairs={{0,4},{1,13},{2,6},{3,15},{4,8},{5,1},{6,10},{7,3},{8,12},{9,5},{1... | collective-permute-start | bytes 344072 | tf_op jit(solution)/shard_map/ppermute | solution.py:366
  51.0 2.7 %collective-permute-start.12 = (f16[8,1792]{1,0:T(8,128)(2,1)S(1)}, f16[8,1792]{1,0:T(8,128)(2,1)S(1)}, u32[]{:S(2)}, u32[]{:S(2)}) collective-permute-start(f16[8,1792]{1,0:T(8,128)(2,1)S(1)} %multiply_convert_fusion), channel_id=1, source_target_pairs={{0,8},{1,9},{2,10},{3,11},{4,12},{5,13},{6,14},{7,15},{8,0},{9,1},... | collective-permute-start | bytes 86024 | tf_op jit(solution)/shard_map/ppermute | solution.py:366
  53.7 12.7 %collective-permute-done.9 = f16[16,3584]{1,0:T(8,128)(2,1)S(1)} collective-permute-done((f16[16,3584]{1,0:T(8,128)(2,1)S(1)}, f16[16,3584]{1,0:T(8,128)(2,1)S(1)}, u32[]{:S(2)}, u32[]{:S(2)}) %collective-permute-start.9) | collective-permute-done | bytes 114720 | tf_op jit(solution)/shard_map/ppermute | solution.py:366
  66.6 3.0 %collective-permute-done.10 = f16[8,3584]{1,0:T(8,128)(2,1)S(1)} collective-permute-done((f16[8,3584]{1,0:T(8,128)(2,1)S(1)}, f16[8,3584]{1,0:T(8,128)(2,1)S(1)}, u32[]{:S(2)}, u32[]{:S(2)}) %collective-permute-start.10) | collective-permute-done | bytes 57376 | tf_op jit(solution)/shard_map/ppermute | solution.py:366
  69.7 2.7 %collective-permute-start.13 = (f32[4,3584]{1,0:T(4,128)S(1)}, f32[4,3584]{1,0:T(4,128)S(1)}, u32[]{:S(2)}, u32[]{:S(2)}) collective-permute-start(f32[4,3584]{1,0:T(4,128)S(1)} %slice_select_fusion), channel_id=1, source_target_pairs={{0,1},{1,0},{2,3},{3,2},{4,5},{5,4},{6,7},{7,6},{8,9},{9,8},{10,11... | collective-permute-start | bytes 172040 | tf_op jit(solution)/shard_map/ppermute | solution.py:360
  73.0 1.3 %patch_half.1.kept_ref = bf16[4,576,256]{2,1,0:T(8,128)(2,1)} custom-call(s32[3]{0:T(128)S(1)} %copy-done, bf16[576,256]{1,0:T(8,128)(2,1)S(1)} %collective-permute-done.half_ref, bf16[4,576,256]{2,1,0:T(8,128)(2,1)} %get-tuple-element.21.kept_ref), custom_call_target="tpu_custom_call", output_to_operand_aliasing={{}: (2, {})} | custom-call | tf_op jit(solution)/shard_map/patch_half/pallas_call | solution.py:316
  74.3 1.4 %turn.1 = bf16[16,72,128]{2,1,0:T(8,128)(2,1)} custom-call(s32[3]{0:T(128)S(1)} %copy-done.1, bf16[16,72,128]{2,1,0:T(8,128)(2,1)S(1)} %all-to-all-done.pieces_ref), custom_call_target="tpu_custom_call" | custom-call | tf_op jit(solution)/shard_map/turn/pallas_call | solution.py:298
  75.7 4.4 %all-to-all-start.1 = ((bf16[16,72,128]{2,1,0:T(8,128)(2,1)}), bf16[16,72,128]{2,1,0:T(8,128)(2,1)S(1)}, u32[]{:S(2)}, u32[]{:S(2)}) async-start(bf16[16,72,128]{2,1,0:T(8,128)(2,1)} %turn.1), calls=%async_computation.1 | async-start | bytes 589824 | tf_op jit(solution)/shard_map/all_to_all | solution.py:355
  80.8 11.6 %all-to-all-done.1.pieces_ref = bf16[16,72,128]{2,1,0:T(8,128)(2,1)S(1)} async-done(((bf16[16,72,128]{2,1,0:T(8,128)(2,1)}), bf16[16,72,128]{2,1,0:T(8,128)(2,1)S(1)}, u32[]{:S(2)}, u32[]{:S(2)}) %all-to-all-start.1) | async-done | bytes 294944 | tf_op jit(solution)/shard_map/all_to_all | solution.py:355
  92.4 1.4 %patch_pieces.1 = bf16[4,576,256]{2,1,0:T(8,128)(2,1)} custom-call(s32[3]{0:T(128)S(1)} %copy-done.1, bf16[16,72,128]{2,1,0:T(8,128)(2,1)S(1)} %all-to-all-done.1.pieces_ref, bf16[4,576,256]{2,1,0:T(8,128)(2,1)} %patch_half.1.kept_ref), custom_call_target="tpu_custom_call", output_to_operand_aliasing={{}: (2, {})} | custom-call | tf_op jit(solution)/shard_map/patch_pieces/pallas_call | solution.py:342
  (31 shorter events, 4.0 us)
Async XLA Ops:
  1.6 4.2 %collective-permute-start.1 = (bf16[8,3840]{1,0:T(8,128)(2,1)S(1)}, bf16[8,3840]{1,0:T(8,128)(2,1)S(1)}, u32[]{:S(2)}, u32[]{:S(2)}) collective-permute-start(bf16[8,3840]{1,0:T(8,128)(2,1)S(1)} %rows.1), channel_id=1, source_target_pairs={{0,1},{1,0},{2,3},{3,2},{4,5},{5,4},{6,7},{7,6},{8,9},{9,8},{10,11... | collective-permute-start | bytes 184328 | tf_op jit(solution)/shard_map/ppermute | solution.py:360
  5.8 5.2 %collective-permute-start.2 = (bf16[8,3840]{1,0:T(8,128)(2,1)S(1)}, bf16[8,3840]{1,0:T(8,128)(2,1)S(1)}, u32[]{:S(2)}, u32[]{:S(2)}) collective-permute-start(bf16[8,3840]{1,0:T(8,128)(2,1)S(1)} %add.35.own_ref), channel_id=1, source_target_pairs={{0,2},{1,15},{2,4},{3,1},{4,6},{5,3},{6,8},{7,5},{8,10},{9,7},{10,... | collective-permute-start | bytes 184328 | tf_op jit(solution)/shard_map/ppermute | solution.py:366
  11.0 5.6 %collective-permute-start.3 = (bf16[16,3840]{1,0:T(8,128)(2,1)S(1)}, bf16[16,3840]{1,0:T(8,128)(2,1)S(1)}, u32[]{:S(2)}, u32[]{:S(2)}) collective-permute-start(bf16[16,3840]{1,0:T(8,128)(2,1)S(1)} %pad_maximum_fusion), channel_id=1, source_target_pairs={{0,4},{1,13},{2,6},{3,15},{4,8},{5,1},{6,10},{7,3},{8,12},{9,5},{1... | collective-permute-start | bytes 368648 | tf_op jit(solution)/shard_map/ppermute | solution.py:366
  16.6 16.8 %collective-permute-start.6 = (bf16[16,3840]{1,0:T(8,128)(2,1)S(1)}, bf16[16,3840]{1,0:T(8,128)(2,1)S(1)}, u32[]{:S(2)}, u32[]{:S(2)}) collective-permute-start(bf16[16,3840]{1,0:T(8,128)(2,1)S(1)} %collective-permute-done.3.next_ref), channel_id=1, source_target_pairs={{0,1},{1,0},{2,3},{3,2},{4,5},{5,4},{6,7},{7,6},{8,9},{9,8},{10,11... | collective-permute-start | bytes 368648 | tf_op jit(solution)/shard_map/ppermute | solution.py:360
  20.2 6.7 %collective-permute-start.4 = (bf16[8,1920]{1,0:T(8,128)(2,1)S(1)}, bf16[8,1920]{1,0:T(8,128)(2,1)S(1)}, u32[]{:S(2)}, u32[]{:S(2)}) collective-permute-start(bf16[8,1920]{1,0:T(8,128)(2,1)S(1)} %slice_select_fusion.1), channel_id=1, source_target_pairs={{0,8},{1,9},{2,10},{3,11},{4,12},{5,13},{6,14},{7,15},{8,0},{9,1},... | collective-permute-start | bytes 92168 | tf_op jit(solution)/shard_map/ppermute | solution.py:366
  23.9 9.4 %collective-permute-start.5 = (bf16[8,3840]{1,0:T(8,128)(2,1)S(1)}, bf16[8,3840]{1,0:T(8,128)(2,1)S(1)}, u32[]{:S(2)}, u32[]{:S(2)}) collective-permute-start(bf16[8,3840]{1,0:T(8,128)(2,1)S(1)} %collective-permute-done.2.near_ref), channel_id=1, source_target_pairs={{0,1},{1,0},{2,3},{3,2},{4,5},{5,4},{6,7},{7,6},{8,9},{9,8},{10,11... | collective-permute-start | bytes 184328 | tf_op jit(solution)/shard_map/ppermute | solution.py:360
  26.9 6.5 %collective-permute-start.7 = (bf16[8,1920]{1,0:T(8,128)(2,1)S(1)}, bf16[8,1920]{1,0:T(8,128)(2,1)S(1)}, u32[]{:S(2)}, u32[]{:S(2)}) collective-permute-start(bf16[8,1920]{1,0:T(8,128)(2,1)S(1)} %collective-permute-done.4.far_ref), channel_id=1, source_target_pairs={{0,1},{1,0},{2,3},{3,2},{4,5},{5,4},{6,7},{7,6},{8,9},{9,8},{10,11... | collective-permute-start | bytes 92168 | tf_op jit(solution)/shard_map/ppermute | solution.py:360
  36.4 43.7 %copy-start.2 = (bf16[4,3584]{1,0:T(4,128)(2,1)S(1)}, bf16[4,3584]{1,0:T(4,128)(2,1)}, u32[]{:S(2)}) copy-start(bf16[4,3584]{1,0:T(4,128)(2,1)} %hidden_ref.1) | copy-start | bytes 86020
  36.4 10.8 %collective-permute-start.8 = (f32[24,3584]{1,0:T(8,128)S(1)}, f32[24,3584]{1,0:T(8,128)S(1)}, u32[]{:S(2)}, u32[]{:S(2)}) collective-permute-start(f32[24,3584]{1,0:T(8,128)S(1)} %get-tuple-element.26), channel_id=1, source_target_pairs={{0,1},{1,0},{2,3},{3,2},{4,5},{5,4},{6,7},{7,6},{8,9},{9,8},{10,11... | collective-permute-start | bytes 1032200 | tf_op jit(solution)/shard_map/ppermute | solution.py:360
  39.3 35.0 %copy-start.1 = (s32[3]{0:T(128)S(1)}, s32[3]{0:T(128)}, u32[]{:S(2)}) copy-start(s32[3]{0:T(128)} %get-tuple-element.18.info_ref) | copy-start | bytes 40
  39.3 33.0 %collective-permute-start = (bf16[576,256]{1,0:T(8,128)(2,1)S(1)}, bf16[576,256]{1,0:T(8,128)(2,1)S(1)}, u32[]{:S(2)}, u32[]{:S(2)}) collective-permute-start(bf16[576,256]{1,0:T(8,128)(2,1)S(1)} %get-tuple-element.20), channel_id=1, source_target_pairs={{0,8},{1,9},{2,10},{3,11},{4,12},{5,13},{6,14},{7,15},{8,0},{9,1},... | collective-permute-start | bytes 884744 | tf_op jit(solution)/shard_map/ppermute | solution.py:39
  42.7 31.6 %all-to-all-start = ((bf16[16,72,128]{2,1,0:T(8,128)(2,1)}), bf16[16,72,128]{2,1,0:T(8,128)(2,1)S(1)}, u32[]{:S(2)}, u32[]{:S(2)}) async-start(bf16[16,72,128]{2,1,0:T(8,128)(2,1)} %get-tuple-element.19), calls=%async_computation | async-start | bytes 589824 | tf_op jit(solution)/shard_map/all_to_all | solution.py:355
  47.0 4.0 %collective-permute-start.11 = (f32[8,1792]{1,0:T(8,128)S(1)}, f32[8,1792]{1,0:T(8,128)S(1)}, u32[]{:S(2)}, u32[]{:S(2)}) collective-permute-start(f32[8,1792]{1,0:T(8,128)S(1)} %get-tuple-element.28), channel_id=1, source_target_pairs={{0,1},{1,0},{2,3},{3,2},{4,5},{5,4},{6,7},{7,6},{8,9},{9,8},{10,11... | collective-permute-start | bytes 172040 | tf_op jit(solution)/shard_map/ppermute | solution.py:360
  47.2 19.2 %collective-permute-start.9 = (f16[16,3584]{1,0:T(8,128)(2,1)S(1)}, f16[16,3584]{1,0:T(8,128)(2,1)S(1)}, u32[]{:S(2)}, u32[]{:S(2)}) collective-permute-start(f16[16,3584]{1,0:T(8,128)(2,1)S(1)} %fusion.1), channel_id=1, source_target_pairs={{0,4},{1,13},{2,6},{3,15},{4,8},{5,1},{6,10},{7,3},{8,12},{9,5},{1... | collective-permute-start | bytes 344072 | tf_op jit(solution)/shard_map/ppermute | solution.py:366
  51.0 15.6 %collective-permute-start.12 = (f16[8,1792]{1,0:T(8,128)(2,1)S(1)}, f16[8,1792]{1,0:T(8,128)(2,1)S(1)}, u32[]{:S(2)}, u32[]{:S(2)}) collective-permute-start(f16[8,1792]{1,0:T(8,128)(2,1)S(1)} %multiply_convert_fusion), channel_id=1, source_target_pairs={{0,8},{1,9},{2,10},{3,11},{4,12},{5,13},{6,14},{7,15},{8,0},{9,1},... | collective-permute-start | bytes 86024 | tf_op jit(solution)/shard_map/ppermute | solution.py:366
  66.5 3.1 %collective-permute-start.10 = (f16[8,3584]{1,0:T(8,128)(2,1)S(1)}, f16[8,3584]{1,0:T(8,128)(2,1)S(1)}, u32[]{:S(2)}, u32[]{:S(2)}) collective-permute-start(f16[8,3584]{1,0:T(8,128)(2,1)S(1)} %fusion.4), channel_id=1, source_target_pairs={{0,2},{1,15},{2,4},{3,1},{4,6},{5,3},{6,8},{7,5},{8,10},{9,7},{10,... | collective-permute-start | bytes 172040 | tf_op jit(solution)/shard_map/ppermute | solution.py:366
  69.7 10.5 %collective-permute-start.13 = (f32[4,3584]{1,0:T(4,128)S(1)}, f32[4,3584]{1,0:T(4,128)S(1)}, u32[]{:S(2)}, u32[]{:S(2)}) collective-permute-start(f32[4,3584]{1,0:T(4,128)S(1)} %slice_select_fusion), channel_id=1, source_target_pairs={{0,1},{1,0},{2,3},{3,2},{4,5},{5,4},{6,7},{7,6},{8,9},{9,8},{10,11... | collective-permute-start | bytes 172040 | tf_op jit(solution)/shard_map/ppermute | solution.py:360
  72.3 0.7 copy-start
  75.7 16.7 %all-to-all-start.1 = ((bf16[16,72,128]{2,1,0:T(8,128)(2,1)}), bf16[16,72,128]{2,1,0:T(8,128)(2,1)S(1)}, u32[]{:S(2)}, u32[]{:S(2)}) async-start(bf16[16,72,128]{2,1,0:T(8,128)(2,1)} %turn.1), calls=%async_computation.1 | async-start | bytes 589824 | tf_op jit(solution)/shard_map/all_to_all | solution.py:355

commit v3 on v2

--- a/solution.py
+++ b/solution.py
@@ -13,6 +13,7 @@
 BUCKETS = 8
 LANES = 128
 MIB = 1 << 20
+AHEAD = 7
 
 softmax_scale = 192.0 ** (-0.5)
 
@@ -142,10 +143,10 @@
 
 
 def attend_kernel(
-    lengths_ref, queries_ref, cache_ref, up_ref, down_ref,
-    attn_ref, kept_ref, up_out, down_out,
+    lengths_ref, queries_ref, cache_ref,
+    attn_ref, kept_ref,
     queries_buf, cache_buf, attn_buf, lengths_buf,
-    in_sems, kept_sems, attn_sems, weight_sems, lengths_sem,
+    in_sems, kept_sems, attn_sems, lengths_sem,
 ):
     own_rows = queries_buf.shape[0]
     me = lax.axis_index("dev")
@@ -158,15 +159,10 @@
         )
         for r in range(own_rows)
     ]
-    out_copies = [
-        pltpu.make_async_copy(up_ref, up_out, weight_sems.at[0]),
-        pltpu.make_async_copy(down_ref, down_out, weight_sems.at[1]),
-    ]
+    out_copies = []
     for pair in in_copies:
         for copy in pair:
             copy.start()
-    for copy in out_copies:
-        copy.start()
     lengths_copy.wait()
     for r in range(own_rows):
         for copy in in_copies[r]:
@@ -183,18 +179,16 @@
         copy.wait()
 
 
-def attend(lengths, queries, cache, w_up, w_down):
+def attend(lengths, queries, cache):
     own_rows, heads, _ = queries.shape
     return pl.pallas_call(
         attend_kernel,
         out_shape=(
             jax.ShapeDtypeStruct((own_rows, heads, VL), jnp.bfloat16),
             jax.ShapeDtypeStruct(cache.shape, cache.dtype),
-            pltpu.VMEM(w_up.shape, w_up.dtype),
-            pltpu.VMEM(w_down.shape, w_down.dtype),
         ),
-        in_specs=[whole(HBM)] * 5,
-        out_specs=(whole(HBM),) * 2 + (whole(VMEM),) * 2,
+        in_specs=[whole(HBM)] * 3,
+        out_specs=(whole(HBM),) * 2,
         scratch_shapes=[
             pltpu.VMEM(queries.shape, queries.dtype),
             pltpu.VMEM(cache.shape, cache.dtype),
@@ -203,22 +197,39 @@
             pltpu.SemaphoreType.DMA((2 * own_rows,)),
             pltpu.SemaphoreType.DMA((own_rows,)),
             pltpu.SemaphoreType.DMA((own_rows,)),
-            pltpu.SemaphoreType.DMA((2,)),
             pltpu.SemaphoreType.DMA,
         ],
         compiler_params=pltpu.CompilerParams(vmem_limit_bytes=12 * MIB),
         name="attend",
-    )(in_hbm(lengths), in_hbm(queries), in_hbm(cache), in_hbm(w_up), in_hbm(w_down))
+    )(in_hbm(lengths), in_hbm(queries), in_hbm(cache))
 
 
 def feed_kernel(
     up_ref, down_ref,
     own_ref, near_ref, next_ref, far_ref, other_near_ref, other_next_ref, other_far_ref,
     own_out, give_out, keep_out, give_far_out, keep_far_out, load_ref,
-    rows_buf,
+    rows_buf, up_buf, down_buf, sems,
 ):
-    features, _ = up_ref.shape
-    columns = features // 7
+    pieces, depth, _ = up_buf.shape
+    columns = down_buf.shape[2]
+    features = pieces * depth
+    copies = [
+        pltpu.make_async_copy(up_ref.at[pl.ds(i * depth, depth), :], up_buf.at[i], sems.at[i])
+        for i in range(pieces)
+    ] + [
+        pltpu.make_async_copy(
+            down_ref.at[:, pl.ds(i * columns, columns)], down_buf.at[i], sems.at[pieces + i]
+        )
+        for i in range(pieces)
+    ]
+    for copy in copies[:AHEAD]:
+        copy.start()
+
+    def arrive(i):
+        copies[i].wait()
+        if i + AHEAD < len(copies):
+            copies[i + AHEAD].start()
+
     first_core = lax.axis_index("dev") % 2 == 0
     block = own_ref.shape[0]
     width = own_ref.shape[1]
@@ -232,12 +243,21 @@
     rows_buf[7 * block :, width // 2 :] = jnp.where(first_core, other_far, far)
     counts = rows_buf[:, features : features + LANES].astype(jnp.float32)
     load_ref[...] = jnp.sum(counts, axis=0)[0:BUCKETS]
-    up = jnp.dot(rows_buf[:, 0:features], up_ref[...], preferred_element_type=jnp.float32)
+    up = None
+    for i in range(pieces):
+        arrive(i)
+        term = jnp.dot(
+            rows_buf[:, i * depth : (i + 1) * depth],
+            up_buf[i],
+            preferred_element_type=jnp.float32,
+        )
+        up = term if up is None else up + term
     hidden = (up / (1.0 + jnp.exp(-up))).astype(jnp.bfloat16)
     half = features // 2
-    for i in range(features // columns):
+    for i in range(pieces):
+        arrive(pieces + i)
         at = slice(i * columns, (i + 1) * columns)
-        product = jnp.dot(hidden, down_ref[:, at], preferred_element_type=jnp.float32)
+        product = jnp.dot(hidden, down_buf[i], preferred_element_type=jnp.float32)
         own_out[:, at] = product[0:block]
         give_out[:, at] = product[block : 4 * block]
         keep_out[:, at] = product[4 * block : 7 * block]
@@ -259,7 +279,8 @@
 
 
 def feed(w_up, w_down, parts):
-    features, _ = w_up.shape
+    features, units = w_up.shape
+    pieces = 7
     block, row_width = parts[0].shape
     wide = lambda rows, columns: pltpu.VMEM((rows, columns), jnp.float32)
     return pl.pallas_call(
@@ -272,12 +293,17 @@
             wide(block, features // 2),
             jax.ShapeDtypeStruct((BUCKETS,), jnp.float32),
         ),
-        in_specs=[whole(VMEM)] * 9,
+        in_specs=[whole(HBM)] * 2 + [whole(VMEM)] * 7,
         out_specs=(whole(VMEM),) * 6,
-        scratch_shapes=[pltpu.VMEM((8 * block, row_width), jnp.bfloat16)],
-        compiler_params=pltpu.CompilerParams(vmem_limit_bytes=12 * MIB),
+        scratch_shapes=[
+            pltpu.VMEM((8 * block, row_width), jnp.bfloat16),
+            pltpu.VMEM((pieces, features // pieces, units), w_up.dtype),
+            pltpu.VMEM((pieces, units, features // pieces), w_down.dtype),
+            pltpu.SemaphoreType.DMA((2 * pieces,)),
+        ],
+        compiler_params=pltpu.CompilerParams(vmem_limit_bytes=20 * MIB),
         name="feed",
-    )(in_vmem(w_up), in_vmem(w_down), *parts)
+    )(in_hbm(w_up), in_hbm(w_down), *parts)
 
 
 def turn_kernel(devices, info_ref, pieces_ref, out_ref, sems):
@@ -397,7 +423,7 @@
     other_near = swapped(near)
     other_far = swapped(far)
     other_next = swapped(nxt)
-    attn_out, kept, w_up, w_down = attend(lengths, q_lat, cache, w_up, w_down)
+    attn_out, kept = attend(lengths, q_lat, cache)
     own_sums, give, keep, give_far, keep_far, load = feed(
         w_up, w_down, (own, near, nxt, far, other_near, other_next, other_far)
     )
@@ -405,18 +431,20 @@
     got_far = swapped(give_far)
     got = swapped(give)
     sums_far = outward(narrow(keep_far + got_far), 4)
-    sums_next = outward(narrow(keep[block:] + got[block:]), 2)
+    pair_sums = keep + got
+    near_sums = jnp.concatenate([pair_sums[:block], pair_sums[2 * block :]], axis=0)
+    sums_near = outward(narrow(near_sums), 1)
     pieces = exchange(pieces)
     kept = patch_half(info, half, kept)
-    near_sums = keep[:block] + got[:block] + widen(sums_next[block:])
-    sums_near = outward(narrow(near_sums), 1)
+    next_sums = pair_sums[block : 2 * block] + widen(sums_near[block:])
+    sums_next = outward(narrow(next_sums), 2)
     wide_far = widen(sums_far)
     zeros = jnp.zeros_like(wide_far)
     both = jnp.concatenate(
         [jnp.where(first_core, wide_far, zeros), jnp.where(first_core, zeros, wide_far)],
         axis=1,
     )
-    total = own_sums + widen(sums_next[:block]) + widen(sums_near) + both
+    total = own_sums + widen(sums_near[:block]) + widen(sums_next) + both
     low, high = total[:own_rows], total[own_rows:]
     got_total = swapped(jnp.where(first_core, high, low))
     summed = jnp.where(first_core, low, high) + got_total

time: 94.2 us -> 100 us (1.062)
  waiting for transfers between devices: 35.4 us -> 39 us
  starting transfers between devices: 40.4 us -> 42.7 us
    ppermute x6, starting transfers between devices: 16.6 us -> 13.7 us  [outward(): return lax.ppermute(value, 'dev', pairs)]
    ppermute x6, waiting for transfers between devices: 22.9 us -> 25.2 us  [outward(): return lax.ppermute(value, 'dev', pairs)]
    pallas_call x1, Pallas kernels: 3 us -> 5.13 us  [feed(): pl.pallas_call(feed_kernel, out_shape=(wide(block, features), wide(3 * bl...]
    ppermute x7, starting transfers between devices: 11.7 us -> 13.8 us  [swapped(): return lax.ppermute(value, 'dev', [(s, s ^ 1) for s in range(count)])]
    ppermute x1, starting transfers between devices: 3.39 us -> 5.26 us  [shifted(): return lax.ppermute(value, axis, pairs)]
    pallas_call x1, Pallas kernels: 4.83 us -> 3.54 us  [attend(): pl.pallas_call(attend_kernel, out_shape=(jax.ShapeDtypeStruct((own_rows,...]
    ppermute x7, waiting for transfers between devices: 0.91 us -> 2.2 us  [swapped(): return lax.ppermute(value, 'dev', [(s, s ^ 1) for s in range(count)])]
    all_to_all x2, starting transfers between devices: 8.72 us -> 9.94 us  [exchange(): return lax.all_to_all(value, 'dev', 0, 0, tiled=True)]
  transfers between devices with their start and end apart: 16 -> 16, of which waited for: 7 -> 9; matrix products, arithmetic and copies ran while one was open for 1% -> 1% of each run, Pallas kernels for 11% -> 9%
where the time goes in v3:
time: 100 us; the launch traced here: 99.8 us
  starting transfers between devices  42.7 us (43%)
  waiting for transfers between devices  39 us (39%)
  Pallas kernels  16.4 us (16%)
    ppermute x6, waiting for transfers between devices, outward(): return lax.ppermute(value, 'dev', pairs)  25.2 us
    ppermute x7, starting transfers between devices, swapped(): return lax.ppermute(value, 'dev', [(s, s ^ 1) for s in range(count)])  13.8 us
    ppermute x6, starting transfers between devices, outward(): return lax.ppermute(value, 'dev', pairs)  13.7 us
    all_to_all x2, waiting for transfers between devices, exchange(): return lax.all_to_all(value, 'dev', 0, 0, tiled=True)  11.6 us
    all_to_all x2, starting transfers between devices, exchange(): return lax.all_to_all(value, 'dev', 0, 0, tiled=True)  9.94 us
    ppermute x1, starting transfers between devices, shifted(): return lax.ppermute(value, axis, pairs)  5.26 us
    pallas_call x1, Pallas kernels, feed(): pl.pallas_call(feed_kernel, out_shape=(wide(block, features), wide(3 * bl...  5.13 us
    pallas_call x1, Pallas kernels, attend(): pl.pallas_call(attend_kernel, out_shape=(jax.ShapeDtypeStruct((own_rows,...  3.54 us
  transfers between devices with their start and end apart: 16, of which 9 were waited for; matrix products, arithmetic and copies ran while one was open for 1% of the time, Pallas kernels for 9%

profile of v3, /device:TPU:1, one launch (start us, length us, event | category | flops | bytes accessed | tf_op | source)
XLA Modules:
  0.0 99.8 jit_solution(15744995988743621184)
XLA Ops:
  1.6 3.3 %collective-permute-start.1 = (bf16[8,3840]{1,0:T(8,128)(2,1)S(1)}, bf16[8,3840]{1,0:T(8,128)(2,1)S(1)}, u32[]{:S(2)}, u32[]{:S(2)}) collective-permute-start(bf16[8,3840]{1,0:T(8,128)(2,1)S(1)} %rows.1), channel_id=1, source_target_pairs={{0,1},{1,0},{2,3},{3,2},{4,5},{5,4},{6,7},{7,6},{8,9},{9,8},{10,11... | collective-permute-start | bytes 184328 | tf_op jit(solution)/shard_map/ppermute | solution.py:386
  5.8 3.9 %collective-permute-start.2 = (bf16[8,3840]{1,0:T(8,128)(2,1)S(1)}, bf16[8,3840]{1,0:T(8,128)(2,1)S(1)}, u32[]{:S(2)}, u32[]{:S(2)}) collective-permute-start(bf16[8,3840]{1,0:T(8,128)(2,1)S(1)} %add.32.own_ref), channel_id=1, source_target_pairs={{0,2},{1,15},{2,4},{3,1},{4,6},{5,3},{6,8},{7,5},{8,10},{9,7},{10,... | collective-permute-start | bytes 184328 | tf_op jit(solution)/shard_map/ppermute | solution.py:392
  9.7 1.3 %collective-permute-done.2.near_ref = bf16[8,3840]{1,0:T(8,128)(2,1)S(1)} collective-permute-done((bf16[8,3840]{1,0:T(8,128)(2,1)S(1)}, bf16[8,3840]{1,0:T(8,128)(2,1)S(1)}, u32[]{:S(2)}, u32[]{:S(2)}) %collective-permute-start.2) | collective-permute-done | bytes 61472 | tf_op jit(solution)/shard_map/ppermute | solution.py:392
  11.0 2.3 %collective-permute-start.3 = (bf16[16,3840]{1,0:T(8,128)(2,1)S(1)}, bf16[16,3840]{1,0:T(8,128)(2,1)S(1)}, u32[]{:S(2)}, u32[]{:S(2)}) collective-permute-start(bf16[16,3840]{1,0:T(8,128)(2,1)S(1)} %pad_maximum_fusion), channel_id=1, source_target_pairs={{0,4},{1,13},{2,6},{3,15},{4,8},{5,1},{6,10},{7,3},{8,12},{9,5},{1... | collective-permute-start | bytes 368648 | tf_op jit(solution)/shard_map/ppermute | solution.py:392
  13.3 3.3 %collective-permute-done.3.next_ref = bf16[16,3840]{1,0:T(8,128)(2,1)S(1)} collective-permute-done((bf16[16,3840]{1,0:T(8,128)(2,1)S(1)}, bf16[16,3840]{1,0:T(8,128)(2,1)S(1)}, u32[]{:S(2)}, u32[]{:S(2)}) %collective-permute-start.3) | collective-permute-done | bytes 122912 | tf_op jit(solution)/shard_map/ppermute | solution.py:392
  16.6 3.6 %collective-permute-start.6 = (bf16[16,3840]{1,0:T(8,128)(2,1)S(1)}, bf16[16,3840]{1,0:T(8,128)(2,1)S(1)}, u32[]{:S(2)}, u32[]{:S(2)}) collective-permute-start(bf16[16,3840]{1,0:T(8,128)(2,1)S(1)} %collective-permute-done.3.next_ref), channel_id=1, source_target_pairs={{0,1},{1,0},{2,3},{3,2},{4,5},{5,4},{6,7},{7,6},{8,9},{9,8},{10,11... | collective-permute-start | bytes 368648 | tf_op jit(solution)/shard_map/ppermute | solution.py:386
  20.2 3.7 %collective-permute-start.4 = (bf16[8,1920]{1,0:T(8,128)(2,1)S(1)}, bf16[8,1920]{1,0:T(8,128)(2,1)S(1)}, u32[]{:S(2)}, u32[]{:S(2)}) collective-permute-start(bf16[8,1920]{1,0:T(8,128)(2,1)S(1)} %slice_select_fusion.1), channel_id=1, source_target_pairs={{0,8},{1,9},{2,10},{3,11},{4,12},{5,13},{6,14},{7,15},{8,0},{9,1},... | collective-permute-start | bytes 92168 | tf_op jit(solution)/shard_map/ppermute | solution.py:392
  24.3 2.6 %collective-permute-done.4.far_ref = bf16[8,1920]{1,0:T(8,128)(2,1)S(1)} collective-permute-done((bf16[8,1920]{1,0:T(8,128)(2,1)S(1)}, bf16[8,1920]{1,0:T(8,128)(2,1)S(1)}, u32[]{:S(2)}, u32[]{:S(2)}) %collective-permute-start.4) | collective-permute-done | bytes 30752 | tf_op jit(solution)/shard_map/ppermute | solution.py:392
  26.9 1.7 %collective-permute-start.7 = (bf16[8,1920]{1,0:T(8,128)(2,1)S(1)}, bf16[8,1920]{1,0:T(8,128)(2,1)S(1)}, u32[]{:S(2)}, u32[]{:S(2)}) collective-permute-start(bf16[8,1920]{1,0:T(8,128)(2,1)S(1)} %collective-permute-done.4.far_ref), channel_id=1, source_target_pairs={{0,1},{1,0},{2,3},{3,2},{4,5},{5,4},{6,7},{7,6},{8,9},{9,8},{10,11... | collective-permute-start | bytes 92168 | tf_op jit(solution)/shard_map/ppermute | solution.py:386
  29.4 5.1 %feed.1 = (f32[8,3584]{1,0:T(8,128)S(1)}, f32[24,3584]{1,0:T(8,128)S(1)}, f32[24,3584]{1,0:T(8,128)S(1)}, f32[8,1792]{1,0:T(8,128)S(1)}, f32[8,1792]{1,0:T(8,128)S(1)}, /*index=5*/f32[8]{0:T(128)}) custom-call(bf16[3584,640]{1,0:T(8,128)(2,1)} %up_ref.1, bf16[640,3584]{1,0:T(8,128)(2,1)} %down_ref.1, bf16[8,3840]{1,0:T(8,128)(2,1)S(1)} %add.32.own_ref, ...), custom_call_target="tpu_custom_call" | custom-call | tf_op jit(solution)/shard_map/feed/pallas_call | solution.py:286
  35.0 2.7 %payload.1 = (bf16[576,256]{1,0:T(8,128)(2,1)S(1)}, bf16[16,72,128]{2,1,0:T(8,128)(2,1)}, s32[3]{0:T(128)}) custom-call(s32[3,32]{1,0:T(4,128)} %bitcast.6, bf16[4,576,256]{2,1,0:T(8,128)(2,1)} %bitcast.3), custom_call_target="tpu_custom_call" | custom-call | tf_op jit(solution)/shard_map/payload/pallas_call | solution.py:115
  37.7 5.0 %all-to-all-start = ((bf16[16,72,128]{2,1,0:T(8,128)(2,1)}), bf16[16,72,128]{2,1,0:T(8,128)(2,1)S(1)}, u32[]{:S(2)}, u32[]{:S(2)}) async-start(bf16[16,72,128]{2,1,0:T(8,128)(2,1)} %get-tuple-element.17), calls=%async_computation | async-start | bytes 589824 | tf_op jit(solution)/shard_map/all_to_all | solution.py:381
  42.7 5.3 %collective-permute-start = (bf16[576,256]{1,0:T(8,128)(2,1)S(1)}, bf16[576,256]{1,0:T(8,128)(2,1)S(1)}, u32[]{:S(2)}, u32[]{:S(2)}) collective-permute-start(bf16[576,256]{1,0:T(8,128)(2,1)S(1)} %get-tuple-element.18), channel_id=1, source_target_pairs={{0,8},{1,9},{2,10},{3,11},{4,12},{5,13},{6,14},{7,15},{8,0},{9,1},... | collective-permute-start | bytes 884744 | tf_op jit(solution)/shard_map/ppermute | solution.py:40
  49.6 2.1 %collective-permute-start.12 = (f16[8,1792]{1,0:T(8,128)(2,1)S(1)}, f16[8,1792]{1,0:T(8,128)(2,1)S(1)}, u32[]{:S(2)}, u32[]{:S(2)}) collective-permute-start(f16[8,1792]{1,0:T(8,128)(2,1)S(1)} %multiply_convert_fusion), channel_id=1, source_target_pairs={{0,8},{1,9},{2,10},{3,11},{4,12},{5,13},{6,14},{7,15},{8,0},{9,1},... | collective-permute-start | bytes 86024 | tf_op jit(solution)/shard_map/ppermute | solution.py:392
  51.6 15.0 %collective-permute-done.9 = f16[16,3584]{1,0:T(8,128)(2,1)S(1)} collective-permute-done((f16[16,3584]{1,0:T(8,128)(2,1)S(1)}, f16[16,3584]{1,0:T(8,128)(2,1)S(1)}, u32[]{:S(2)}, u32[]{:S(2)}) %collective-permute-start.9) | collective-permute-done | bytes 114720 | tf_op jit(solution)/shard_map/ppermute | solution.py:392
  66.7 1.3 %collective-permute-start.10 = (f16[8,3584]{1,0:T(8,128)(2,1)S(1)}, f16[8,3584]{1,0:T(8,128)(2,1)S(1)}, u32[]{:S(2)}, u32[]{:S(2)}) collective-permute-start(f16[8,3584]{1,0:T(8,128)(2,1)S(1)} %fusion.2), channel_id=1, source_target_pairs={{0,4},{1,13},{2,6},{3,15},{4,8},{5,1},{6,10},{7,3},{8,12},{9,5},{1... | collective-permute-start | bytes 172040 | tf_op jit(solution)/shard_map/ppermute | solution.py:392
  68.0 3.0 %collective-permute-done.10 = f16[8,3584]{1,0:T(8,128)(2,1)S(1)} collective-permute-done((f16[8,3584]{1,0:T(8,128)(2,1)S(1)}, f16[8,3584]{1,0:T(8,128)(2,1)S(1)}, u32[]{:S(2)}, u32[]{:S(2)}) %collective-permute-start.10) | collective-permute-done | bytes 57376 | tf_op jit(solution)/shard_map/ppermute | solution.py:392
  71.1 3.8 %collective-permute-start.13 = (f32[4,3584]{1,0:T(4,128)S(1)}, f32[4,3584]{1,0:T(4,128)S(1)}, u32[]{:S(2)}, u32[]{:S(2)}) collective-permute-start(f32[4,3584]{1,0:T(4,128)S(1)} %slice_select_fusion), channel_id=1, source_target_pairs={{0,1},{1,0},{2,3},{3,2},{4,5},{5,4},{6,7},{7,6},{8,9},{9,8},{10,11... | collective-permute-start | bytes 172040 | tf_op jit(solution)/shard_map/ppermute | solution.py:386
  74.9 3.5 %attend.1 = (bf16[4,64,512]{2,1,0:T(8,128)(2,1)}, bf16[4,576,256]{2,1,0:T(8,128)(2,1)}) custom-call(s32[64]{0:T(128)} %lengths_ref.1, bf16[4,64,576]{2,1,0:T(8,128)(2,1)} %queries_ref.1, bf16[4,576,256]{2,1,0:T(8,128)(2,1)} %bitcast.4), custom_call_target="tpu_custom_call" | custom-call | tf_op jit(solution)/shard_map/attend/pallas_call | solution.py:184
  78.5 1.3 %patch_half.1.kept_ref = bf16[4,576,256]{2,1,0:T(8,128)(2,1)} custom-call(s32[3]{0:T(128)S(1)} %copy-done, bf16[576,256]{1,0:T(8,128)(2,1)S(1)} %collective-permute-done.half_ref, bf16[4,576,256]{2,1,0:T(8,128)(2,1)} %get-tuple-element.19.kept_ref), custom_call_target="tpu_custom_call", output_to_operand_aliasing={{}: (2, {})} | custom-call | tf_op jit(solution)/shard_map/patch_half/pallas_call | solution.py:342
  79.8 1.4 %turn.1 = bf16[16,72,128]{2,1,0:T(8,128)(2,1)} custom-call(s32[3]{0:T(128)S(1)} %copy-done, bf16[16,72,128]{2,1,0:T(8,128)(2,1)S(1)} %all-to-all-done.pieces_ref), custom_call_target="tpu_custom_call" | custom-call | tf_op jit(solution)/shard_map/turn/pallas_call | solution.py:324
  81.2 4.9 %all-to-all-start.1 = ((bf16[16,72,128]{2,1,0:T(8,128)(2,1)}), bf16[16,72,128]{2,1,0:T(8,128)(2,1)S(1)}, u32[]{:S(2)}, u32[]{:S(2)}) async-start(bf16[16,72,128]{2,1,0:T(8,128)(2,1)} %turn.1), calls=%async_computation.1 | async-start | bytes 589824 | tf_op jit(solution)/shard_map/all_to_all | solution.py:381
  86.8 11.6 %all-to-all-done.1.pieces_ref = bf16[16,72,128]{2,1,0:T(8,128)(2,1)S(1)} async-done(((bf16[16,72,128]{2,1,0:T(8,128)(2,1)}), bf16[16,72,128]{2,1,0:T(8,128)(2,1)S(1)}, u32[]{:S(2)}, u32[]{:S(2)}) %all-to-all-start.1) | async-done | bytes 294944 | tf_op jit(solution)/shard_map/all_to_all | solution.py:381
  98.4 1.4 %patch_pieces.1 = bf16[4,576,256]{2,1,0:T(8,128)(2,1)} custom-call(s32[3]{0:T(128)S(1)} %copy-done, bf16[16,72,128]{2,1,0:T(8,128)(2,1)S(1)} %all-to-all-done.1.pieces_ref, bf16[4,576,256]{2,1,0:T(8,128)(2,1)} %patch_half.1.kept_ref), custom_call_target="tpu_custom_call", output_to_operand_aliasing={{}: (2, {})} | custom-call | tf_op jit(solution)/shard_map/patch_pieces/pallas_call | solution.py:368
  (31 shorter events, 5.9 us)
Async XLA Ops:
  1.6 4.2 %collective-permute-start.1 = (bf16[8,3840]{1,0:T(8,128)(2,1)S(1)}, bf16[8,3840]{1,0:T(8,128)(2,1)S(1)}, u32[]{:S(2)}, u32[]{:S(2)}) collective-permute-start(bf16[8,3840]{1,0:T(8,128)(2,1)S(1)} %rows.1), channel_id=1, source_target_pairs={{0,1},{1,0},{2,3},{3,2},{4,5},{5,4},{6,7},{7,6},{8,9},{9,8},{10,11... | collective-permute-start | bytes 184328 | tf_op jit(solution)/shard_map/ppermute | solution.py:386
  5.8 5.2 %collective-permute-start.2 = (bf16[8,3840]{1,0:T(8,128)(2,1)S(1)}, bf16[8,3840]{1,0:T(8,128)(2,1)S(1)}, u32[]{:S(2)}, u32[]{:S(2)}) collective-permute-start(bf16[8,3840]{1,0:T(8,128)(2,1)S(1)} %add.32.own_ref), channel_id=1, source_target_pairs={{0,2},{1,15},{2,4},{3,1},{4,6},{5,3},{6,8},{7,5},{8,10},{9,7},{10,... | collective-permute-start | bytes 184328 | tf_op jit(solution)/shard_map/ppermute | solution.py:392
  11.0 5.6 %collective-permute-start.3 = (bf16[16,3840]{1,0:T(8,128)(2,1)S(1)}, bf16[16,3840]{1,0:T(8,128)(2,1)S(1)}, u32[]{:S(2)}, u32[]{:S(2)}) collective-permute-start(bf16[16,3840]{1,0:T(8,128)(2,1)S(1)} %pad_maximum_fusion), channel_id=1, source_target_pairs={{0,4},{1,13},{2,6},{3,15},{4,8},{5,1},{6,10},{7,3},{8,12},{9,5},{1... | collective-permute-start | bytes 368648 | tf_op jit(solution)/shard_map/ppermute | solution.py:392
  16.6 12.8 %collective-permute-start.6 = (bf16[16,3840]{1,0:T(8,128)(2,1)S(1)}, bf16[16,3840]{1,0:T(8,128)(2,1)S(1)}, u32[]{:S(2)}, u32[]{:S(2)}) collective-permute-start(bf16[16,3840]{1,0:T(8,128)(2,1)S(1)} %collective-permute-done.3.next_ref), channel_id=1, source_target_pairs={{0,1},{1,0},{2,3},{3,2},{4,5},{5,4},{6,7},{7,6},{8,9},{9,8},{10,11... | collective-permute-start | bytes 368648 | tf_op jit(solution)/shard_map/ppermute | solution.py:386
  20.2 6.7 %collective-permute-start.4 = (bf16[8,1920]{1,0:T(8,128)(2,1)S(1)}, bf16[8,1920]{1,0:T(8,128)(2,1)S(1)}, u32[]{:S(2)}, u32[]{:S(2)}) collective-permute-start(bf16[8,1920]{1,0:T(8,128)(2,1)S(1)} %slice_select_fusion.1), channel_id=1, source_target_pairs={{0,8},{1,9},{2,10},{3,11},{4,12},{5,13},{6,14},{7,15},{8,0},{9,1},... | collective-permute-start | bytes 92168 | tf_op jit(solution)/shard_map/ppermute | solution.py:392
  23.9 5.5 %collective-permute-start.5 = (bf16[8,3840]{1,0:T(8,128)(2,1)S(1)}, bf16[8,3840]{1,0:T(8,128)(2,1)S(1)}, u32[]{:S(2)}, u32[]{:S(2)}) collective-permute-start(bf16[8,3840]{1,0:T(8,128)(2,1)S(1)} %collective-permute-done.2.near_ref), channel_id=1, source_target_pairs={{0,1},{1,0},{2,3},{3,2},{4,5},{5,4},{6,7},{7,6},{8,9},{9,8},{10,11... | collective-permute-start | bytes 184328 | tf_op jit(solution)/shard_map/ppermute | solution.py:386
  26.9 2.5 %collective-permute-start.7 = (bf16[8,1920]{1,0:T(8,128)(2,1)S(1)}, bf16[8,1920]{1,0:T(8,128)(2,1)S(1)}, u32[]{:S(2)}, u32[]{:S(2)}) collective-permute-start(bf16[8,1920]{1,0:T(8,128)(2,1)S(1)} %collective-permute-done.4.far_ref), channel_id=1, source_target_pairs={{0,1},{1,0},{2,3},{3,2},{4,5},{5,4},{6,7},{7,6},{8,9},{9,8},{10,11... | collective-permute-start | bytes 92168 | tf_op jit(solution)/shard_map/ppermute | solution.py:386
  34.5 14.2 %collective-permute-start.8 = (f32[24,3584]{1,0:T(8,128)S(1)}, f32[24,3584]{1,0:T(8,128)S(1)}, u32[]{:S(2)}, u32[]{:S(2)}) collective-permute-start(f32[24,3584]{1,0:T(8,128)S(1)} %get-tuple-element.22), channel_id=1, source_target_pairs={{0,1},{1,0},{2,3},{3,2},{4,5},{5,4},{6,7},{7,6},{8,9},{9,8},{10,11... | collective-permute-start | bytes 1032200 | tf_op jit(solution)/shard_map/ppermute | solution.py:386
  37.7 42.1 %all-to-all-start = ((bf16[16,72,128]{2,1,0:T(8,128)(2,1)}), bf16[16,72,128]{2,1,0:T(8,128)(2,1)S(1)}, u32[]{:S(2)}, u32[]{:S(2)}) async-start(bf16[16,72,128]{2,1,0:T(8,128)(2,1)} %get-tuple-element.17), calls=%async_computation | async-start | bytes 589824 | tf_op jit(solution)/shard_map/all_to_all | solution.py:381
  42.7 35.7 %collective-permute-start = (bf16[576,256]{1,0:T(8,128)(2,1)S(1)}, bf16[576,256]{1,0:T(8,128)(2,1)S(1)}, u32[]{:S(2)}, u32[]{:S(2)}) collective-permute-start(bf16[576,256]{1,0:T(8,128)(2,1)S(1)} %get-tuple-element.18), channel_id=1, source_target_pairs={{0,8},{1,9},{2,10},{3,11},{4,12},{5,13},{6,14},{7,15},{8,0},{9,1},... | collective-permute-start | bytes 884744 | tf_op jit(solution)/shard_map/ppermute | solution.py:40
  48.0 1.6 %collective-permute-start.11 = (f32[8,1792]{1,0:T(8,128)S(1)}, f32[8,1792]{1,0:T(8,128)S(1)}, u32[]{:S(2)}, u32[]{:S(2)}) collective-permute-start(f32[8,1792]{1,0:T(8,128)S(1)} %get-tuple-element.24), channel_id=1, source_target_pairs={{0,1},{1,0},{2,3},{3,2},{4,5},{5,4},{6,7},{7,6},{8,9},{9,8},{10,11... | collective-permute-start | bytes 172040 | tf_op jit(solution)/shard_map/ppermute | solution.py:386
  48.8 17.9 %collective-permute-start.9 = (f16[16,3584]{1,0:T(8,128)(2,1)S(1)}, f16[16,3584]{1,0:T(8,128)(2,1)S(1)}, u32[]{:S(2)}, u32[]{:S(2)}) collective-permute-start(f16[16,3584]{1,0:T(8,128)(2,1)S(1)} %fusion), channel_id=1, source_target_pairs={{0,2},{1,15},{2,4},{3,1},{4,6},{5,3},{6,8},{7,5},{8,10},{9,7},{10,... | collective-permute-start | bytes 344072 | tf_op jit(solution)/shard_map/ppermute | solution.py:392
  49.6 18.4 %collective-permute-start.12 = (f16[8,1792]{1,0:T(8,128)(2,1)S(1)}, f16[8,1792]{1,0:T(8,128)(2,1)S(1)}, u32[]{:S(2)}, u32[]{:S(2)}) collective-permute-start(f16[8,1792]{1,0:T(8,128)(2,1)S(1)} %multiply_convert_fusion), channel_id=1, source_target_pairs={{0,8},{1,9},{2,10},{3,11},{4,12},{5,13},{6,14},{7,15},{8,0},{9,1},... | collective-permute-start | bytes 86024 | tf_op jit(solution)/shard_map/ppermute | solution.py:392
  66.7 11.8 %copy-start = (s32[3]{0:T(128)S(1)}, s32[3]{0:T(128)}, u32[]{:S(2)}) copy-start(s32[3]{0:T(128)} %get-tuple-element.16.info_ref) | copy-start | bytes 40
  66.7 4.3 %collective-permute-start.10 = (f16[8,3584]{1,0:T(8,128)(2,1)S(1)}, f16[8,3584]{1,0:T(8,128)(2,1)S(1)}, u32[]{:S(2)}, u32[]{:S(2)}) collective-permute-start(f16[8,3584]{1,0:T(8,128)(2,1)S(1)} %fusion.2), channel_id=1, source_target_pairs={{0,4},{1,13},{2,6},{3,15},{4,8},{5,1},{6,10},{7,3},{8,12},{9,5},{1... | collective-permute-start | bytes 172040 | tf_op jit(solution)/shard_map/ppermute | solution.py:392
  71.1 15.0 %collective-permute-start.13 = (f32[4,3584]{1,0:T(4,128)S(1)}, f32[4,3584]{1,0:T(4,128)S(1)}, u32[]{:S(2)}, u32[]{:S(2)}) collective-permute-start(f32[4,3584]{1,0:T(4,128)S(1)} %slice_select_fusion), channel_id=1, source_target_pairs={{0,1},{1,0},{2,3},{3,2},{4,5},{5,4},{6,7},{7,6},{8,9},{9,8},{10,11... | collective-permute-start | bytes 172040 | tf_op jit(solution)/shard_map/ppermute | solution.py:386
  79.8 6.3 %copy-start.1 = (bf16[4,3584]{1,0:T(4,128)(2,1)S(1)}, bf16[4,3584]{1,0:T(4,128)(2,1)}, u32[]{:S(2)}) copy-start(bf16[4,3584]{1,0:T(4,128)(2,1)} %hidden_ref.1) | copy-start | bytes 86020
  81.2 17.2 %all-to-all-start.1 = ((bf16[16,72,128]{2,1,0:T(8,128)(2,1)}), bf16[16,72,128]{2,1,0:T(8,128)(2,1)S(1)}, u32[]{:S(2)}, u32[]{:S(2)}) async-start(bf16[16,72,128]{2,1,0:T(8,128)(2,1)} %turn.1), calls=%async_computation.1 | async-start | bytes 589824 | tf_op jit(solution)/shard_map/all_to_all | solution.py:381

commit v4 on v3

--- a/solution.py
+++ b/solution.py
@@ -206,8 +206,8 @@
 
 def feed_kernel(
     up_ref, down_ref,
-    own_ref, near_ref, next_ref, far_ref, other_near_ref, other_next_ref, other_far_ref,
-    own_out, give_out, keep_out, give_far_out, keep_far_out, load_ref,
+    own_ref, near_ref, next_ref, far_ref, other_ref, other_far_ref,
+    own_out, give_out, keep_out, keep_far_out, load_ref,
     rows_buf, up_buf, down_buf, sems,
 ):
     pieces, depth, _ = up_buf.shape
@@ -234,7 +234,7 @@
     block = own_ref.shape[0]
     width = own_ref.shape[1]
     for at, part in (
-        (0, own_ref), (1, near_ref), (2, next_ref), (4, other_near_ref), (5, other_next_ref),
+        (0, own_ref), (1, near_ref), (2, next_ref), (4, other_ref),
     ):
         rows_buf[at * block : at * block + part.shape[0], :] = part[...]
     far = far_ref[...]
@@ -259,7 +259,7 @@
         at = slice(i * columns, (i + 1) * columns)
         product = jnp.dot(hidden, down_buf[i], preferred_element_type=jnp.float32)
         own_out[:, at] = product[0:block]
-        give_out[:, at] = product[block : 4 * block]
+        give_out[0 : 3 * block, at] = product[block : 4 * block]
         keep_out[:, at] = product[4 * block : 7 * block]
         far_sums = product[7 * block :]
         for low, high in ((0, half), (half, features)):
@@ -275,7 +275,7 @@
 
                 @pl.when(jnp.logical_not(mine))
                 def _(piece=piece, target=target):
-                    give_far_out[:, target] = piece
+                    give_out[3 * block :, target] = piece
 
 
 def feed(w_up, w_down, parts):
@@ -287,14 +287,13 @@
         feed_kernel,
         out_shape=(
             wide(block, features),
+            wide(4 * block, features),
             wide(3 * block, features),
-            wide(3 * block, features),
-            wide(block, features // 2),
             wide(block, features // 2),
             jax.ShapeDtypeStruct((BUCKETS,), jnp.float32),
         ),
-        in_specs=[whole(HBM)] * 2 + [whole(VMEM)] * 7,
-        out_specs=(whole(VMEM),) * 6,
+        in_specs=[whole(HBM)] * 2 + [whole(VMEM)] * 6,
+        out_specs=(whole(VMEM),) * 5,
         scratch_shapes=[
             pltpu.VMEM((8 * block, row_width), jnp.bfloat16),
             pltpu.VMEM((pieces, features // pieces, units), w_up.dtype),
@@ -407,7 +406,7 @@
     q_lat, latent_cache, lengths, moves, hidden_in, norm_gain, w_up, w_down, queue_counts, deadline
 ):
     devices = lax.axis_size("dev")
-    own_rows, _ = hidden_in.shape
+    own_rows, features = hidden_in.shape
     first_core = lax.axis_index("dev") % 2 == 0
     block = 2 * own_rows
     cache = jnp.swapaxes(latent_cache, 1, 2)
@@ -420,16 +419,15 @@
     pieces = exchange(pieces)
     nxt = outward(jnp.concatenate([own, near], axis=0), 2)
     half = shifted(half, "dev", devices // 2)
-    other_near = swapped(near)
     other_far = swapped(far)
-    other_next = swapped(nxt)
+    other = swapped(jnp.concatenate([near, nxt], axis=0))
     attn_out, kept = attend(lengths, q_lat, cache)
-    own_sums, give, keep, give_far, keep_far, load = feed(
-        w_up, w_down, (own, near, nxt, far, other_near, other_next, other_far)
+    own_sums, give, keep, keep_far, load = feed(
+        w_up, w_down, (own, near, nxt, far, other, other_far)
     )
     pieces = turn(info, pieces)
-    got_far = swapped(give_far)
     got = swapped(give)
+    got, got_far = got[: 3 * block], got[3 * block :, : features // 2]
     sums_far = outward(narrow(keep_far + got_far), 4)
     pair_sums = keep + got
     near_sums = jnp.concatenate([pair_sums[:block], pair_sums[2 * block :]], axis=0)

time: 100 us -> 81.9 us (0.82)
  waiting for transfers between devices: 39 us -> 20.5 us
    all_to_all x2, waiting for transfers between devices: 11.6 us -> 0.01 us  [exchange(): return lax.all_to_all(value, 'dev', 0, 0, tiled=True)]
    ppermute x6, starting transfers between devices: 13.7 us -> 22.4 us  [outward(): return lax.ppermute(value, 'dev', pairs)]
    ppermute x7 -> x5, starting transfers between devices: 13.8 us -> 7.3 us  [swapped(): return lax.ppermute(value, 'dev', [(s, s ^ 1) for s in range(count)])]
    ppermute x6, waiting for transfers between devices: 25.2 us -> 18.8 us  [outward(): return lax.ppermute(value, 'dev', pairs)]
    ppermute x1, starting transfers between devices: 5.26 us -> 0.15 us  [shifted(): return lax.ppermute(value, axis, pairs)]
    all_to_all x2, starting transfers between devices: 9.94 us -> 13 us  [exchange(): return lax.all_to_all(value, 'dev', 0, 0, tiled=True)]
    ppermute x7 -> x5, waiting for transfers between devices: 2.2 us -> 1.76 us  [swapped(): return lax.ppermute(value, 'dev', [(s, s ^ 1) for s in range(count)])]
  transfers between devices with their start and end apart: 16 -> 14, of which waited for: 9 -> 6; matrix products, arithmetic and copies ran while one was open for 1% -> 0% of each run, Pallas kernels for 9% -> 19%
where the time goes in v4:
time: 81.9 us; the launch traced here: 81.5 us
  starting transfers between devices  42.8 us (52%)
  waiting for transfers between devices  20.5 us (25%)
  Pallas kernels  16.4 us (20%)
  other arithmetic  0.88 us (1%)
    ppermute x6, starting transfers between devices, outward(): return lax.ppermute(value, 'dev', pairs)  22.4 us
    ppermute x6, waiting for transfers between devices, outward(): return lax.ppermute(value, 'dev', pairs)  18.8 us
    all_to_all x2, starting transfers between devices, exchange(): return lax.all_to_all(value, 'dev', 0, 0, tiled=True)  13 us
    ppermute x5, starting transfers between devices, swapped(): return lax.ppermute(value, 'dev', [(s, s ^ 1) for s in range(count)])  7.3 us
    pallas_call x1, Pallas kernels, feed(): pl.pallas_call(feed_kernel, out_shape=(wide(block, features), wide(4 * bl...  5.13 us
    pallas_call x1, Pallas kernels, attend(): pl.pallas_call(attend_kernel, out_shape=(jax.ShapeDtypeStruct((own_rows,...  3.54 us
    pallas_call x1, Pallas kernels, make_payload(): pl.pallas_call(partial(payload_kernel, devices), out_shape=(pltpu.VMEM((d...  2.73 us
    ppermute x5, waiting for transfers between devices, swapped(): return lax.ppermute(value, 'dev', [(s, s ^ 1) for s in range(count)])  1.76 us
  transfers between devices with their start and end apart: 14, of which 6 were waited for; matrix products, arithmetic and copies ran while one was open for 0% of the time, Pallas kernels for 19%

profile of v4, /device:TPU:1, one launch (start us, length us, event | category | flops | bytes accessed | tf_op | source)
XLA Modules:
  0.0 81.5 jit_solution(11543615559010068466)
XLA Ops:
  0.6 0.9 %rows.1 = bf16[8,3840]{1,0:T(8,128)(2,1)S(1)} custom-call(bf16[4,3584]{1,0:T(4,128)(2,1)} %hidden_ref.1, bf16[3584]{0:T(1024)(128)(2,1)} %gain_ref.1, s32[1,8]{1,0:T(1,128)} %queue_ref.1, s32[4]{0:T(128)} %deadline_ref.1), custom_call_target="tpu_custom_call" | custom-call | tf_op jit(solution)/shard_map/rows/pallas_call | solution.py:77
  1.6 3.3 %collective-permute-start.1 = (bf16[8,3840]{1,0:T(8,128)(2,1)S(1)}, bf16[8,3840]{1,0:T(8,128)(2,1)S(1)}, u32[]{:S(2)}, u32[]{:S(2)}) collective-permute-start(bf16[8,3840]{1,0:T(8,128)(2,1)S(1)} %rows.1), channel_id=1, source_target_pairs={{0,1},{1,0},{2,3},{3,2},{4,5},{5,4},{6,7},{7,6},{8,9},{9,8},{10,11... | collective-permute-start | bytes 184328 | tf_op jit(solution)/shard_map/ppermute | solution.py:385
  4.9 0.9 %collective-permute-done.1 = bf16[8,3840]{1,0:T(8,128)(2,1)S(1)} collective-permute-done((bf16[8,3840]{1,0:T(8,128)(2,1)S(1)}, bf16[8,3840]{1,0:T(8,128)(2,1)S(1)}, u32[]{:S(2)}, u32[]{:S(2)}) %collective-permute-start.1) | collective-permute-done | bytes 61472 | tf_op jit(solution)/shard_map/ppermute | solution.py:385
  5.8 3.9 %collective-permute-start.2 = (bf16[8,3840]{1,0:T(8,128)(2,1)S(1)}, bf16[8,3840]{1,0:T(8,128)(2,1)S(1)}, u32[]{:S(2)}, u32[]{:S(2)}) collective-permute-start(bf16[8,3840]{1,0:T(8,128)(2,1)S(1)} %add.32.own_ref), channel_id=1, source_target_pairs={{0,2},{1,15},{2,4},{3,1},{4,6},{5,3},{6,8},{7,5},{8,10},{9,7},{10,... | collective-permute-start | bytes 184328 | tf_op jit(solution)/shard_map/ppermute | solution.py:391
  9.7 1.3 %collective-permute-done.2.near_ref = bf16[8,3840]{1,0:T(8,128)(2,1)S(1)} collective-permute-done((bf16[8,3840]{1,0:T(8,128)(2,1)S(1)}, bf16[8,3840]{1,0:T(8,128)(2,1)S(1)}, u32[]{:S(2)}, u32[]{:S(2)}) %collective-permute-start.2) | collective-permute-done | bytes 61472 | tf_op jit(solution)/shard_map/ppermute | solution.py:391
  11.0 2.3 %collective-permute-start.3 = (bf16[16,3840]{1,0:T(8,128)(2,1)S(1)}, bf16[16,3840]{1,0:T(8,128)(2,1)S(1)}, u32[]{:S(2)}, u32[]{:S(2)}) collective-permute-start(bf16[16,3840]{1,0:T(8,128)(2,1)S(1)} %pad_maximum_fusion.1), channel_id=1, source_target_pairs={{0,4},{1,13},{2,6},{3,15},{4,8},{5,1},{6,10},{7,3},{8,12},{9,5},{1... | collective-permute-start | bytes 368648 | tf_op jit(solution)/shard_map/ppermute | solution.py:391
  13.3 2.7 %payload.1 = (bf16[576,256]{1,0:T(8,128)(2,1)S(1)}, bf16[16,72,128]{2,1,0:T(8,128)(2,1)}, s32[3]{0:T(128)}) custom-call(s32[3,32]{1,0:T(4,128)} %bitcast.6, bf16[4,576,256]{2,1,0:T(8,128)(2,1)} %bitcast.3), custom_call_target="tpu_custom_call" | custom-call | tf_op jit(solution)/shard_map/payload/pallas_call | solution.py:115
  16.1 5.7 %all-to-all-start = ((bf16[16,72,128]{2,1,0:T(8,128)(2,1)}), bf16[16,72,128]{2,1,0:T(8,128)(2,1)S(1)}, u32[]{:S(2)}, u32[]{:S(2)}) async-start(bf16[16,72,128]{2,1,0:T(8,128)(2,1)} %get-tuple-element.16), calls=%async_computation | async-start | bytes 589824 | tf_op jit(solution)/shard_map/all_to_all | solution.py:380
  22.1 5.6 %collective-permute-start.4 = (bf16[8,1920]{1,0:T(8,128)(2,1)S(1)}, bf16[8,1920]{1,0:T(8,128)(2,1)S(1)}, u32[]{:S(2)}, u32[]{:S(2)}) collective-permute-start(bf16[8,1920]{1,0:T(8,128)(2,1)S(1)} %slice_select_fusion.1), channel_id=1, source_target_pairs={{0,8},{1,9},{2,10},{3,11},{4,12},{5,13},{6,14},{7,15},{8,0},{9,1},... | collective-permute-start | bytes 92168 | tf_op jit(solution)/shard_map/ppermute | solution.py:391
  27.7 7.7 %collective-permute-done.4.far_ref = bf16[8,1920]{1,0:T(8,128)(2,1)S(1)} collective-permute-done((bf16[8,1920]{1,0:T(8,128)(2,1)S(1)}, bf16[8,1920]{1,0:T(8,128)(2,1)S(1)}, u32[]{:S(2)}, u32[]{:S(2)}) %collective-permute-start.4) | collective-permute-done | bytes 30752 | tf_op jit(solution)/shard_map/ppermute | solution.py:391
  35.4 0.7 collective-permute-start.6
  36.1 0.9 %collective-permute-done.6.other_far_ref = bf16[8,1920]{1,0:T(8,128)(2,1)S(1)} collective-permute-done((bf16[8,1920]{1,0:T(8,128)(2,1)S(1)}, bf16[8,1920]{1,0:T(8,128)(2,1)S(1)}, u32[]{:S(2)}, u32[]{:S(2)}) %collective-permute-start.6) | collective-permute-done | bytes 30752 | tf_op jit(solution)/shard_map/ppermute | solution.py:385
  37.0 5.1 %feed.1 = (f32[8,3584]{1,0:T(8,128)S(1)}, f32[32,3584]{1,0:T(8,128)S(1)}, f32[24,3584]{1,0:T(8,128)S(1)}, f32[8,1792]{1,0:T(8,128)S(1)}, f32[8]{0:T(128)}) custom-call(bf16[3584,640]{1,0:T(8,128)(2,1)} %up_ref.1, bf16[640,3584]{1,0:T(8,128)(2,1)} %down_ref.1, bf16[8,3840]{1,0:T(8,128)(2,1)S(1)} %add.32.own_ref, ...), custom_call_target="tpu_custom_call" | custom-call | tf_op jit(solution)/shard_map/feed/pallas_call | solution.py:286
  42.7 1.4 %turn.1 = bf16[16,72,128]{2,1,0:T(8,128)(2,1)} custom-call(s32[3]{0:T(128)S(1)} %copy-done, bf16[16,72,128]{2,1,0:T(8,128)(2,1)S(1)} %all-to-all-done.pieces_ref), custom_call_target="tpu_custom_call" | custom-call | tf_op jit(solution)/shard_map/turn/pallas_call | solution.py:323
  44.1 7.2 %all-to-all-start.1 = ((bf16[16,72,128]{2,1,0:T(8,128)(2,1)}), bf16[16,72,128]{2,1,0:T(8,128)(2,1)S(1)}, u32[]{:S(2)}, u32[]{:S(2)}) async-start(bf16[16,72,128]{2,1,0:T(8,128)(2,1)} %turn.1), calls=%async_computation.1 | async-start | bytes 589824 | tf_op jit(solution)/shard_map/all_to_all | solution.py:380
  51.5 2.6 %collective-permute-start.8 = (f16[16,3584]{1,0:T(8,128)(2,1)S(1)}, f16[16,3584]{1,0:T(8,128)(2,1)S(1)}, u32[]{:S(2)}, u32[]{:S(2)}) collective-permute-start(f16[16,3584]{1,0:T(8,128)(2,1)S(1)} %fusion), channel_id=1, source_target_pairs={{0,2},{1,15},{2,4},{3,1},{4,6},{5,3},{6,8},{7,5},{8,10},{9,7},{10,... | collective-permute-start | bytes 344072 | tf_op jit(solution)/shard_map/ppermute | solution.py:391
  54.2 3.1 %collective-permute-start.10 = (f16[8,1792]{1,0:T(8,128)(2,1)S(1)}, f16[8,1792]{1,0:T(8,128)(2,1)S(1)}, u32[]{:S(2)}, u32[]{:S(2)}) collective-permute-start(f16[8,1792]{1,0:T(8,128)(2,1)S(1)} %fusion.4), channel_id=1, source_target_pairs={{0,8},{1,9},{2,10},{3,11},{4,12},{5,13},{6,14},{7,15},{8,0},{9,1},... | collective-permute-start | bytes 86024 | tf_op jit(solution)/shard_map/ppermute | solution.py:391
  57.2 8.1 %collective-permute-done.8 = f16[16,3584]{1,0:T(8,128)(2,1)S(1)} collective-permute-done((f16[16,3584]{1,0:T(8,128)(2,1)S(1)}, f16[16,3584]{1,0:T(8,128)(2,1)S(1)}, u32[]{:S(2)}, u32[]{:S(2)}) %collective-permute-start.8) | collective-permute-done | bytes 114720 | tf_op jit(solution)/shard_map/ppermute | solution.py:391
  65.3 4.8 %collective-permute-start.9 = (f16[8,3584]{1,0:T(8,128)(2,1)S(1)}, f16[8,3584]{1,0:T(8,128)(2,1)S(1)}, u32[]{:S(2)}, u32[]{:S(2)}) collective-permute-start(f16[8,3584]{1,0:T(8,128)(2,1)S(1)} %fusion.2), channel_id=1, source_target_pairs={{0,4},{1,13},{2,6},{3,15},{4,8},{5,1},{6,10},{7,3},{8,12},{9,5},{1... | collective-permute-start | bytes 172040 | tf_op jit(solution)/shard_map/ppermute | solution.py:391
  70.1 1.7 %collective-permute-done.9 = f16[8,3584]{1,0:T(8,128)(2,1)S(1)} collective-permute-done((f16[8,3584]{1,0:T(8,128)(2,1)S(1)}, f16[8,3584]{1,0:T(8,128)(2,1)S(1)}, u32[]{:S(2)}, u32[]{:S(2)}) %collective-permute-start.9) | collective-permute-done | bytes 57376 | tf_op jit(solution)/shard_map/ppermute | solution.py:391
  71.9 2.6 %collective-permute-start.11 = (f32[4,3584]{1,0:T(4,128)S(1)}, f32[4,3584]{1,0:T(4,128)S(1)}, u32[]{:S(2)}, u32[]{:S(2)}) collective-permute-start(f32[4,3584]{1,0:T(4,128)S(1)} %slice_select_fusion), channel_id=1, source_target_pairs={{0,1},{1,0},{2,3},{3,2},{4,5},{5,4},{6,7},{7,6},{8,9},{9,8},{10,11... | collective-permute-start | bytes 172040 | tf_op jit(solution)/shard_map/ppermute | solution.py:385
  74.5 3.5 %attend.1 = (bf16[4,64,512]{2,1,0:T(8,128)(2,1)}, bf16[4,576,256]{2,1,0:T(8,128)(2,1)}) custom-call(s32[64]{0:T(128)} %lengths_ref.1, bf16[4,64,576]{2,1,0:T(8,128)(2,1)} %queries_ref.1, bf16[4,576,256]{2,1,0:T(8,128)(2,1)} %bitcast.4), custom_call_target="tpu_custom_call" | custom-call | tf_op jit(solution)/shard_map/attend/pallas_call | solution.py:184
  78.1 1.3 %patch_half.1.kept_ref = bf16[4,576,256]{2,1,0:T(8,128)(2,1)} custom-call(s32[3]{0:T(128)S(1)} %copy-done, bf16[576,256]{1,0:T(8,128)(2,1)S(1)} %collective-permute-done.half_ref, bf16[4,576,256]{2,1,0:T(8,128)(2,1)} %get-tuple-element.18.kept_ref), custom_call_target="tpu_custom_call", output_to_operand_aliasing={{}: (2, {})} | custom-call | tf_op jit(solution)/shard_map/patch_half/pallas_call | solution.py:341
  79.4 1.4 %patch_pieces.1 = bf16[4,576,256]{2,1,0:T(8,128)(2,1)} custom-call(s32[3]{0:T(128)S(1)} %copy-done, bf16[16,72,128]{2,1,0:T(8,128)(2,1)S(1)} %all-to-all-done.1.pieces_ref, bf16[4,576,256]{2,1,0:T(8,128)(2,1)} %patch_half.1.kept_ref), custom_call_target="tpu_custom_call", output_to_operand_aliasing={{}: (2, {})} | custom-call | tf_op jit(solution)/shard_map/patch_pieces/pallas_call | solution.py:367
  (28 shorter events, 1.7 us)
Async XLA Ops:
  1.6 4.2 %collective-permute-start.1 = (bf16[8,3840]{1,0:T(8,128)(2,1)S(1)}, bf16[8,3840]{1,0:T(8,128)(2,1)S(1)}, u32[]{:S(2)}, u32[]{:S(2)}) collective-permute-start(bf16[8,3840]{1,0:T(8,128)(2,1)S(1)} %rows.1), channel_id=1, source_target_pairs={{0,1},{1,0},{2,3},{3,2},{4,5},{5,4},{6,7},{7,6},{8,9},{9,8},{10,11... | collective-permute-start | bytes 184328 | tf_op jit(solution)/shard_map/ppermute | solution.py:385
  5.8 5.2 %collective-permute-start.2 = (bf16[8,3840]{1,0:T(8,128)(2,1)S(1)}, bf16[8,3840]{1,0:T(8,128)(2,1)S(1)}, u32[]{:S(2)}, u32[]{:S(2)}) collective-permute-start(bf16[8,3840]{1,0:T(8,128)(2,1)S(1)} %add.32.own_ref), channel_id=1, source_target_pairs={{0,2},{1,15},{2,4},{3,1},{4,6},{5,3},{6,8},{7,5},{8,10},{9,7},{10,... | collective-permute-start | bytes 184328 | tf_op jit(solution)/shard_map/ppermute | solution.py:391
  11.0 10.8 %collective-permute-start.3 = (bf16[16,3840]{1,0:T(8,128)(2,1)S(1)}, bf16[16,3840]{1,0:T(8,128)(2,1)S(1)}, u32[]{:S(2)}, u32[]{:S(2)}) collective-permute-start(bf16[16,3840]{1,0:T(8,128)(2,1)S(1)} %pad_maximum_fusion.1), channel_id=1, source_target_pairs={{0,4},{1,13},{2,6},{3,15},{4,8},{5,1},{6,10},{7,3},{8,12},{9,5},{1... | collective-permute-start | bytes 368648 | tf_op jit(solution)/shard_map/ppermute | solution.py:391
  16.1 26.6 %all-to-all-start = ((bf16[16,72,128]{2,1,0:T(8,128)(2,1)}), bf16[16,72,128]{2,1,0:T(8,128)(2,1)S(1)}, u32[]{:S(2)}, u32[]{:S(2)}) async-start(bf16[16,72,128]{2,1,0:T(8,128)(2,1)} %get-tuple-element.16), calls=%async_computation | async-start | bytes 589824 | tf_op jit(solution)/shard_map/all_to_all | solution.py:380
  21.9 15.1 %collective-permute-start.5 = (bf16[24,3840]{1,0:T(8,128)(2,1)S(1)}, bf16[24,3840]{1,0:T(8,128)(2,1)S(1)}, u32[]{:S(2)}, u32[]{:S(2)}) collective-permute-start(bf16[24,3840]{1,0:T(8,128)(2,1)S(1)} %pad_maximum_fusion), channel_id=1, source_target_pairs={{0,1},{1,0},{2,3},{3,2},{4,5},{5,4},{6,7},{7,6},{8,9},{9,8},{10,11... | collective-permute-start | bytes 552968 | tf_op jit(solution)/shard_map/ppermute | solution.py:385
  22.1 20.7 %copy-start = (s32[3]{0:T(128)S(1)}, s32[3]{0:T(128)}, u32[]{:S(2)}) copy-start(s32[3]{0:T(128)} %get-tuple-element.15.info_ref) | copy-start | bytes 40
  22.1 13.3 %collective-permute-start.4 = (bf16[8,1920]{1,0:T(8,128)(2,1)S(1)}, bf16[8,1920]{1,0:T(8,128)(2,1)S(1)}, u32[]{:S(2)}, u32[]{:S(2)}) collective-permute-start(bf16[8,1920]{1,0:T(8,128)(2,1)S(1)} %slice_select_fusion.1), channel_id=1, source_target_pairs={{0,8},{1,9},{2,10},{3,11},{4,12},{5,13},{6,14},{7,15},{8,0},{9,1},... | collective-permute-start | bytes 92168 | tf_op jit(solution)/shard_map/ppermute | solution.py:391
  35.4 1.6 %collective-permute-start.6 = (bf16[8,1920]{1,0:T(8,128)(2,1)S(1)}, bf16[8,1920]{1,0:T(8,128)(2,1)S(1)}, u32[]{:S(2)}, u32[]{:S(2)}) collective-permute-start(bf16[8,1920]{1,0:T(8,128)(2,1)S(1)} %collective-permute-done.4.far_ref), channel_id=1, source_target_pairs={{0,1},{1,0},{2,3},{3,2},{4,5},{5,4},{6,7},{7,6},{8,9},{9,8},{10,11... | collective-permute-start | bytes 92168 | tf_op jit(solution)/shard_map/ppermute | solution.py:385
  42.1 9.3 %collective-permute-start.7 = (f32[32,3584]{1,0:T(8,128)S(1)}, f32[32,3584]{1,0:T(8,128)S(1)}, u32[]{:S(2)}, u32[]{:S(2)}) collective-permute-start(f32[32,3584]{1,0:T(8,128)S(1)} %get-tuple-element.21), channel_id=1, source_target_pairs={{0,1},{1,0},{2,3},{3,2},{4,5},{5,4},{6,7},{7,6},{8,9},{9,8},{10,11... | collective-permute-start | bytes 1376264 | tf_op jit(solution)/shard_map/ppermute | solution.py:385
  42.6 35.5 %collective-permute-start = (bf16[576,256]{1,0:T(8,128)(2,1)S(1)}, bf16[576,256]{1,0:T(8,128)(2,1)S(1)}, u32[]{:S(2)}, u32[]{:S(2)}) collective-permute-start(bf16[576,256]{1,0:T(8,128)(2,1)S(1)} %get-tuple-element.17), channel_id=1, source_target_pairs={{0,8},{1,9},{2,10},{3,11},{4,12},{5,13},{6,14},{7,15},{8,0},{9,1},... | collective-permute-start | bytes 884744 | tf_op jit(solution)/shard_map/ppermute | solution.py:40
  44.1 35.3 %all-to-all-start.1 = ((bf16[16,72,128]{2,1,0:T(8,128)(2,1)}), bf16[16,72,128]{2,1,0:T(8,128)(2,1)S(1)}, u32[]{:S(2)}, u32[]{:S(2)}) async-start(bf16[16,72,128]{2,1,0:T(8,128)(2,1)} %turn.1), calls=%async_computation.1 | async-start | bytes 589824 | tf_op jit(solution)/shard_map/all_to_all | solution.py:380
  51.5 13.8 %collective-permute-start.8 = (f16[16,3584]{1,0:T(8,128)(2,1)S(1)}, f16[16,3584]{1,0:T(8,128)(2,1)S(1)}, u32[]{:S(2)}, u32[]{:S(2)}) collective-permute-start(f16[16,3584]{1,0:T(8,128)(2,1)S(1)} %fusion), channel_id=1, source_target_pairs={{0,2},{1,15},{2,4},{3,1},{4,6},{5,3},{6,8},{7,5},{8,10},{9,7},{10,... | collective-permute-start | bytes 344072 | tf_op jit(solution)/shard_map/ppermute | solution.py:391
  54.2 15.9 %collective-permute-start.10 = (f16[8,1792]{1,0:T(8,128)(2,1)S(1)}, f16[8,1792]{1,0:T(8,128)(2,1)S(1)}, u32[]{:S(2)}, u32[]{:S(2)}) collective-permute-start(f16[8,1792]{1,0:T(8,128)(2,1)S(1)} %fusion.4), channel_id=1, source_target_pairs={{0,8},{1,9},{2,10},{3,11},{4,12},{5,13},{6,14},{7,15},{8,0},{9,1},... | collective-permute-start | bytes 86024 | tf_op jit(solution)/shard_map/ppermute | solution.py:391
  65.3 6.5 %collective-permute-start.9 = (f16[8,3584]{1,0:T(8,128)(2,1)S(1)}, f16[8,3584]{1,0:T(8,128)(2,1)S(1)}, u32[]{:S(2)}, u32[]{:S(2)}) collective-permute-start(f16[8,3584]{1,0:T(8,128)(2,1)S(1)} %fusion.2), channel_id=1, source_target_pairs={{0,4},{1,13},{2,6},{3,15},{4,8},{5,1},{6,10},{7,3},{8,12},{9,5},{1... | collective-permute-start | bytes 172040 | tf_op jit(solution)/shard_map/ppermute | solution.py:391
  71.9 8.9 %collective-permute-start.11 = (f32[4,3584]{1,0:T(4,128)S(1)}, f32[4,3584]{1,0:T(4,128)S(1)}, u32[]{:S(2)}, u32[]{:S(2)}) collective-permute-start(f32[4,3584]{1,0:T(4,128)S(1)} %slice_select_fusion), channel_id=1, source_target_pairs={{0,1},{1,0},{2,3},{3,2},{4,5},{5,4},{6,7},{7,6},{8,9},{9,8},{10,11... | collective-permute-start | bytes 172040 | tf_op jit(solution)/shard_map/ppermute | solution.py:385
  79.4 1.4 %copy-start.1 = (bf16[4,3584]{1,0:T(4,128)(2,1)S(1)}, bf16[4,3584]{1,0:T(4,128)(2,1)}, u32[]{:S(2)}) copy-start(bf16[4,3584]{1,0:T(4,128)(2,1)} %hidden_ref.1) | copy-start | bytes 86020
